TPU v7x, 32 devices: a whole 2x2x4 slice. The times are simulated.
32 devices in a mesh: grp: 8 (over z, y), rep: 4 (over x, core).
Axes of the slice: x: 2, y: 2, z: 4, core: 2. Of those that a mesh axis runs over, the one named last changes fastest.
Arguments:
- queries: bfloat16 [16, 4, 32, 128], P('grp', 'rep'), may hold values from -3.2 to 3.2
- passages: bfloat16 [512, 4, 180, 128], P('grp', 'rep'), may hold values from -1.796875 to 1.796875
- lengths: int32 [512, 4], P('grp', 'rep'), may hold values from 16 to 180
- cand_ids: int32 [16, 4, 64], P('grp', 'rep'), may hold values from 0 to 511, as said below
- owner_map: int32 [4, 512], P('rep'), may hold values from 0 to 511, as said below
- teacher: float32 [16, 4, 64], P('grp', 'rep'), may hold values from -12 to 312
- weights: float32 [16, 4], P('grp', 'rep'), may hold values from 0.5 to 18
Outputs:
- loss: float32 [], replicated
- query_grad: float32 [16, 4, 32, 128], P('grp', 'rep')
- passage_grad: bfloat16 [512, 4, 180, 128], P('grp', 'rep')
Inputs may be any that keep to these rules, and one draw needn't show every extreme that they name: `cand_ids`: within each replica, the 128 candidates of the queries of one grp index have storage rows of which at most 32 (counted with repeats) lie in any one aligned block of 64 rows; in every draw, in each replica, one block receives exactly 32 from every grp index. `owner_map`: each row is a permutation of 0 to 511.
All inputs are finite; a program needn't handle non-finite values.
Results may differ from a plain program's by a relative error of at most 0.0055.
Values may be sent and summed in bfloat16 or wider, within the bound.
No kernel may reach another device: no remote copies, remote signals or barrier semaphores. Data moves between devices by JAX's collectives and lax.ppermute only.
A program may use at most 128 MiB of HBM per device.

v0:
```python
import functools
import math

import jax
import jax.numpy as jnp
from jax import lax
from jax.experimental import pallas as pl
from jax.experimental.pallas import tpu as pltpu
from jax.sharding import PartitionSpec as P

TEMPER = 0.05
LOG2E = math.log2(math.e)
MASKED = -1e30
KINDS = 8
UNROLL = 8
SPREAD = 4
HIGHEST = lax.Precision.HIGHEST
VMEM = pltpu.VMEM
SMEM = pltpu.SMEM


def round_up(value, multiple):
    return -(-value // multiple) * multiple


def iota(shape, dim):
    return lax.broadcasted_iota(jnp.int32, shape, dim)


def three_parts(values):
    first = values.astype(jnp.bfloat16).astype(jnp.float32)
    rest = values - first
    second = rest.astype(jnp.bfloat16).astype(jnp.float32)
    third = (rest - second).astype(jnp.bfloat16).astype(jnp.float32)
    return first, second, third


def pack_kernel(passage_local, queries, cand_ids, owner_map, teacher, weights, out, aux):
    groups = out.shape[0]
    tokens = queries.shape[0]
    query_local, _, candidates = cand_ids.shape
    entries = owner_map.shape[1]
    table = owner_map[...].astype(jnp.float32)
    owner = jnp.floor((table + 0.5) * (1.0 / passage_local))
    local = table - owner * passage_local
    which = iota((8, entries), 0)
    tables = jnp.where(which == 0, owner, jnp.where(which == 1, local, 0.0)).astype(jnp.bfloat16)
    aux[...] = jnp.zeros_like(aux)
    for q in range(query_local):
        hot = (iota((entries, candidates), 0) == cand_ids[q]).astype(jnp.bfloat16)
        found = jnp.dot(tables, hot, preferred_element_type=jnp.float32)
        scores = teacher[q]
        shifted = scores - jnp.max(scores, axis=1, keepdims=True)
        log_teacher = shifted - jnp.log(jnp.sum(jnp.exp(shifted), axis=1, keepdims=True))
        weight = jnp.broadcast_to(weights[:, q : q + 1], (1, candidates))
        rows = (found[0:1], found[1:2], *three_parts(log_teacher), *three_parts(weight))
        for kind, row in enumerate(rows):
            at = kind * query_local + q
            aux[at : at + 1, 0:candidates] = row
    packed = aux[...].astype(jnp.bfloat16)
    for g in range(groups):
        out[g, 0:tokens, :] = queries[...]
        out[g, tokens:, :] = packed


def owned_rows(arrived, tokens, query_local, candidates, g, q, me):
    at = tokens + q
    owner = arrived[g, at : at + 1, 0:candidates].astype(jnp.float32)
    at = tokens + query_local + q
    local = arrived[g, at : at + 1, 0:candidates].astype(jnp.float32)
    return jnp.where(owner == me.astype(jnp.float32), local, -1.0).astype(jnp.int32)


def prepare_kernel(stored, rows_out, gathered):
    token_len, chunk, feature = stored.shape
    padded = rows_out.shape[1]
    pitch = gathered.shape[0] // chunk
    for p in range(chunk):
        at = p * pitch + token_len
        gathered[at : (p + 1) * pitch, :] = jnp.zeros((pitch - token_len, feature), jnp.float32)

    def spread(j, carry):
        for u in range(SPREAD):
            at = j * SPREAD + u
            gathered[pl.ds(at, chunk, stride=pitch), :] = stored[at].astype(jnp.float32)
        return carry

    lax.fori_loop(0, token_len // SPREAD, spread, 0)
    for j in range(token_len - token_len % SPREAD, token_len):
        gathered[pl.ds(j, chunk, stride=pitch), :] = stored[j].astype(jnp.float32)

    for p in range(chunk):
        rows_out[p] = gathered[p * pitch : p * pitch + padded, :].astype(jnp.bfloat16)


def list_blocks(flags_scalar, block_row, block_tile, block_count, passage_count, tiles):
    def list_passage(p, count):
        for tile in range(tiles):
            block_row[0, count] = p
            block_tile[0, count] = tile
            count = count + flags_scalar[p, tile]
        return count

    count = lax.fori_loop(0, passage_count, list_passage, jnp.int32(0))
    for extra in range(3 * UNROLL):
        block_row[0, count + extra] = passage_count
        block_tile[0, count + extra] = 0
    steps = (count + 2 * UNROLL - 1) // (2 * UNROLL)
    block_count[0, 0] = steps
    return steps


def score_kernel(
    dims,
    axis,
    arrived,
    lengths,
    passages_hbm,
    scores_out,
    highest,
    summed,
    weight_sum,
    block_row,
    block_tile,
    block_count,
    powers_hbm,
    passages,
    turned,
    flags,
    flags_scalar,
    penalty,
    even,
    odd,
    even_top,
    odd_top,
    powers,
    flags_done,
    rows_done,
    powers_done,
):
    tokens, query_local, candidates, per_tile = dims
    groups = arrived.shape[0]
    passage_count, padded, feature = passages.shape
    tiles, _, lanes = highest.shape
    me = lax.axis_index(axis)
    groups_per_tile = per_tile // query_local
    fetch_rows = pltpu.make_async_copy(passages_hbm, passages, rows_done)
    fetch_rows.start()

    column = iota(flags.shape, 1)
    passage_index = iota((passage_count, candidates), 0)
    marks = jnp.zeros(flags.shape, jnp.int32)
    for tile in range(tiles):
        hit = jnp.zeros((passage_count, candidates), jnp.int32)
        for g in range(tile * groups_per_tile, (tile + 1) * groups_per_tile):
            for q in range(query_local):
                mine = owned_rows(arrived, tokens, query_local, candidates, g, q, me)
                hit = jnp.where(passage_index == mine, 1, hit)
        any_hit = jnp.max(hit, axis=1, keepdims=True)
        marks = jnp.where(column == tile, any_hit, marks)
    flags[...] = marks
    to_scalar = pltpu.make_async_copy(flags, flags_scalar, flags_done)
    to_scalar.start()

    total = jnp.zeros((1, 1), jnp.float32)
    for g in range(groups):
        for q in range(query_local):
            for part in range(5, 8):
                at = tokens + part * query_local + q
                total = total + arrived[g, at : at + 1, 0:1].astype(jnp.float32)
    weight_sum[...] = jnp.broadcast_to(total, weight_sum.shape)
    for tile in range(tiles):
        parts = [
            arrived[g, 0:tokens, :]
            for g in range(tile * groups_per_tile, (tile + 1) * groups_per_tile)
        ]
        block = jnp.concatenate(parts, axis=0).astype(jnp.float32)
        turned[tile] = block.T.astype(jnp.bfloat16)
    highest[...] = jnp.zeros_like(highest)
    summed[...] = jnp.ones_like(summed)
    penalty[...] = jnp.where(iota(penalty.shape, 0) < padded, 0.0, MASKED)
    to_scalar.wait()
    steps = list_blocks(flags_scalar, block_row, block_tile, block_count, passage_count, tiles)
    fetch_rows.wait()

    factor = LOG2E / TEMPER

    def multiply(first, into, tops):
        for u in range(UNROLL):
            p = jnp.minimum(block_row[0, first + u], passage_count - 1)
            tile = block_tile[0, first + u]
            products = jnp.dot(passages[p], turned[tile], preferred_element_type=jnp.float32)
            products = products + penalty[pl.ds(padded - lengths[0, p], padded), :]
            into[u] = products
            tops[u : u + 1, :] = jnp.max(products, axis=0, keepdims=True)

    def soften(first, held, tops):
        for u in range(UNROLL):
            slot = block_row[0, first + u]
            tile = block_tile[0, first + u]
            top = tops[u : u + 1, :]
            raised = jnp.exp2((held[u] - top) * factor)
            powers[first + u] = raised.astype(jnp.bfloat16)
            highest[tile, pl.ds(slot, 1), :] = top
            summed[tile, pl.ds(slot, 1), :] = jnp.sum(raised, axis=0, keepdims=True)

    def chunk_copy(s):
        at = pl.ds(s * 2 * UNROLL, 2 * UNROLL)
        return pltpu.make_async_copy(powers.at[at], powers_hbm.at[at], powers_done.at[s])

    multiply(0, even, even_top)

    def step(s, carry):
        first = s * 2 * UNROLL
        multiply(first + UNROLL, odd, odd_top)
        soften(first, even, even_top)
        multiply(first + 2 * UNROLL, even, even_top)
        soften(first + UNROLL, odd, odd_top)
        chunk_copy(s).start()
        return carry

    lax.fori_loop(0, steps, step, 0)

    query_len = lanes // per_tile
    member = iota((lanes, 128), 0) // query_len == iota((lanes, 128), 1)
    member = member.astype(jnp.float32)
    scores_out[0] = jnp.zeros(scores_out.shape[1:], jnp.float32)
    for tile in range(tiles):
        matched = highest[tile, 0:passage_count, :] + TEMPER * jnp.log(
            summed[tile, 0:passage_count, :]
        )
        sums = jnp.dot(matched, member, precision=HIGHEST, preferred_element_type=jnp.float32)
        for inner in range(per_tile):
            g = tile * groups_per_tile + inner // query_local
            q = inner % query_local
            mine = owned_rows(arrived, tokens, query_local, candidates, g, q, me)
            picked = jnp.where(passage_index == mine, sums[:, inner : inner + 1], 0.0)
            at = tile * per_tile + inner
            scores_out[0, at : at + 1, 0:candidates] = jnp.sum(picked, axis=0, keepdims=True)
    for g in range(1, groups):
        scores_out[g] = scores_out[0]

    def finish(s, carry):
        chunk_copy(s).wait()
        return carry

    lax.fori_loop(0, steps, finish, 0)


def pair_sums(values):
    while len(values) > 1:
        values = [values[i] + values[i + 1] for i in range(0, len(values), 2)]
    return values[0]


def query_kernel(dims, axis, arrived, scores, summed, *refs):
    tokens, query_local, candidates, per_tile, query_total, replicas = dims
    weight_sums, refs = refs[:replicas], refs[replicas:]
    block_row, block_tile, block_count, passages_hbm, powers_hbm = refs[:5]
    grads_out, multiplier, numerator_out, weight_sum_out = refs[5:9]
    passages, powers, sums, rows_done, powers_done = refs[9:]
    groups = arrived.shape[0]
    tiles, slots, lanes = summed.shape
    passage_count, padded, _ = passages.shape
    groups_per_tile = per_tile // query_local
    queries_all = tiles * per_tile
    query_len = lanes // per_tile
    me = lax.axis_index(axis)
    steps = block_count[0, 0]

    fetch_rows = pltpu.make_async_copy(passages_hbm, passages, rows_done)
    fetch_rows.start()

    def chunk_copy(s):
        at = pl.ds(s * 2 * UNROLL, 2 * UNROLL)
        return pltpu.make_async_copy(powers_hbm.at[at], powers.at[at], powers_done.at[s])

    def fetch(s, carry):
        chunk_copy(s).start()
        return carry

    lax.fori_loop(0, steps, fetch, 0)

    got = scores[0]
    for g in range(1, groups):
        got = got + scores[g]
    student = got[0:queries_all, 0:candidates]

    def gather_parts(kind):
        rows = []
        for g in range(groups):
            parts = []
            for part in range(3):
                at = tokens + (kind + part) * query_local
                block = arrived[g, at : at + query_local, 0:candidates]
                parts.append(block.astype(jnp.float32))
            rows.append((parts[0] + parts[1]) + parts[2])
        return jnp.concatenate(rows, axis=0)

    log_teacher = gather_parts(2)
    weight = gather_parts(5)
    shifted = student - jnp.max(student, axis=1, keepdims=True)
    log_student = shifted - jnp.log(jnp.sum(jnp.exp(shifted), axis=1, keepdims=True))
    teacher_prob = jnp.exp(log_teacher)
    spread = jnp.sum(weight * teacher_prob * (log_teacher - log_student), axis=1, keepdims=True)
    numerator = jnp.sum(spread, axis=0, keepdims=True)
    numerator_out[...] = jnp.broadcast_to(numerator, numerator_out.shape)
    weight_sum = pair_sums([one[...] for one in weight_sums])
    weight_sum_out[...] = weight_sum
    scale = query_total / weight_sum[0:1, 0:1]
    grad = (weight * scale) * (jnp.exp(log_student) - teacher_prob)

    passage_index = iota((passage_count, candidates), 0)
    lane_query = iota((passage_count, lanes), 1) // query_len
    for tile in range(tiles):
        spread_out = jnp.zeros((passage_count, lanes), jnp.float32)
        for inner in range(per_tile):
            g = tile * groups_per_tile + inner // query_local
            q = inner % query_local
            mine = owned_rows(arrived, tokens, query_local, candidates, g, q, me)
            at = tile * per_tile + inner
            picked = jnp.where(passage_index == mine, grad[at : at + 1], 0.0)
            total = jnp.sum(picked, axis=1, keepdims=True)
            spread_out = jnp.where(lane_query == inner, total, spread_out)
        multiplier[tile, 0:passage_count, :] = spread_out / summed[tile, 0:passage_count, :]
        multiplier[tile, passage_count:, :] = jnp.zeros((slots - passage_count, lanes), jnp.float32)

    sums[...] = jnp.zeros_like(sums)
    fetch_rows.wait()

    def step(s, carry):
        chunk_copy(s).wait()
        for u in range(2 * UNROLL):
            b = s * 2 * UNROLL + u
            slot = block_row[0, b]
            tile = block_tile[0, b]
            p = jnp.minimum(slot, passage_count - 1)
            part = powers[b].astype(jnp.float32) * multiplier[tile, pl.ds(slot, 1), :]
            part = part.astype(jnp.bfloat16)
            sums[tile] += lax.dot_general(
                passages[p], part, (((0,), (0,)), ((), ())), preferred_element_type=jnp.float32
            )
        return carry

    lax.fori_loop(0, steps, step, 0)
    for tile in range(tiles):
        back = sums[tile].T.astype(jnp.bfloat16)
        for inner in range(groups_per_tile):
            g = tile * groups_per_tile + inner
            grads_out[g] = back[inner * tokens : (inner + 1) * tokens]


def passage_kernel(
    dims,
    arrived,
    multiplier,
    block_row,
    block_tile,
    block_count,
    powers_hbm,
    out,
    powers,
    sums,
    queries_all,
    powers_done,
):
    tokens, per_tile_groups = dims
    token_len, passage_count, feature = out.shape
    tiles = queries_all.shape[0]
    padded = powers.shape[1]
    pitch = sums.shape[0] // (passage_count + 1)
    steps = block_count[0, 0]

    def chunk_copy(s):
        at = pl.ds(s * 2 * UNROLL, 2 * UNROLL)
        return pltpu.make_async_copy(powers_hbm.at[at], powers.at[at], powers_done.at[s])

    def fetch(s, carry):
        chunk_copy(s).start()
        return carry

    lax.fori_loop(0, steps, fetch, 0)
    for tile in range(tiles):
        for inner in range(per_tile_groups):
            g = tile * per_tile_groups + inner
            queries_all[tile, inner * tokens : (inner + 1) * tokens, :] = arrived[g, 0:tokens, :]

    def clear(p, carry):
        sums[pl.ds(p * pitch, pitch), :] = jnp.zeros((pitch, feature), jnp.float32)
        return carry

    lax.fori_loop(0, passage_count, clear, 0)

    def step(s, carry):
        chunk_copy(s).wait()
        for u in range(2 * UNROLL):
            b = s * 2 * UNROLL + u
            slot = block_row[0, b]
            tile = block_tile[0, b]
            part = powers[b].astype(jnp.float32) * multiplier[tile, pl.ds(slot, 1), :]
            at = pl.ds(pl.multiple_of(slot * pitch, 8), padded)
            sums[at, :] += jnp.dot(
                part.astype(jnp.bfloat16), queries_all[tile], preferred_element_type=jnp.float32
            )
        return carry

    lax.fori_loop(0, steps, step, 0)

    def store(j, carry):
        for u in range(SPREAD):
            at = j * SPREAD + u
            out[at] = sums[pl.ds(at, passage_count, stride=pitch), :].astype(out.dtype)
        return carry

    lax.fori_loop(0, token_len // SPREAD, store, 0)
    for j in range(token_len - token_len % SPREAD, token_len):
        out[j] = sums[pl.ds(j, passage_count, stride=pitch), :].astype(out.dtype)


def vmem(count):
    return [pl.BlockSpec(memory_space=VMEM)] * count


def smem(count):
    return [pl.BlockSpec(memory_space=SMEM)] * count


def from_replicas(values, replicas):
    rings = [[(r, r ^ hop) for r in range(replicas)] for hop in range(1, replicas)]
    return [values] + [lax.ppermute(values, "rep", ring) for ring in rings]


def hbm(count):
    return [pl.BlockSpec(memory_space=pltpu.HBM)] * count


def on_device(queries, passages, lengths, cand_ids, owner_map, teacher, weights):
    groups = lax.axis_size("grp")
    replicas = lax.axis_size("rep")
    query_local, _, query_len, feature = queries.shape
    passage_local, _, token_len, _ = passages.shape
    candidates = cand_ids.shape[2]
    tokens = query_local * query_len
    lanes = 128
    per_tile = lanes // query_len
    tiles = groups * tokens // lanes
    padded = round_up(token_len, 16)
    pitch = round_up(padded, 16) + 8
    ref_count = query_local * candidates
    capacity = groups * (2 * ref_count // groups)
    limit = min(passage_local * tiles, capacity)
    blocks = limit + 3 * UNROLL
    chunks = -(-limit // (2 * UNROLL))
    aux_rows = round_up(KINDS * query_local, 16)
    slots = round_up(passage_local + 1, 8)
    score_rows = round_up(groups * query_local, 8)
    shape = jax.ShapeDtypeStruct
    params = pltpu.CompilerParams(vmem_limit_bytes=62 * 2**20)

    share = pl.pallas_call(
        functools.partial(pack_kernel, passage_local),
        out_shape=shape((groups, tokens + aux_rows, feature), jnp.bfloat16),
        in_specs=vmem(5),
        out_specs=pl.BlockSpec(memory_space=VMEM),
        scratch_shapes=[VMEM((aux_rows, feature), jnp.float32)],
        name="pack",
        compiler_params=params,
    )(queries.reshape(tokens, feature), cand_ids, owner_map, teacher, weights.T)
    arrived = lax.all_to_all(share, "grp", split_axis=0, concat_axis=0, tiled=True)

    chunk = math.gcd(passage_local, 16)
    rows = pl.pallas_call(
        prepare_kernel,
        grid=(passage_local // chunk,),
        out_shape=shape((passage_local, padded, feature), jnp.bfloat16),
        in_specs=[pl.BlockSpec((token_len, chunk, feature), lambda i: (0, i, 0))],
        out_specs=pl.BlockSpec((chunk, padded, feature), lambda i: (i, 0, 0)),
        scratch_shapes=[VMEM((chunk * pitch, feature), jnp.float32)],
        name="prepare",
        compiler_params=params,
    )(passages[:, 0].transpose(1, 0, 2))

    dims = (tokens, query_local, candidates, per_tile)
    scores, highest, summed, weight_sum, block_row, block_tile, block_count, powers = (
        pl.pallas_call(
            functools.partial(score_kernel, dims, "grp"),
            out_shape=(
                shape((groups, score_rows, 128), jnp.float32),
                shape((tiles, slots, lanes), jnp.float32),
                shape((tiles, slots, lanes), jnp.float32),
                shape((1, 128), jnp.float32),
                shape((1, blocks), jnp.int32),
                shape((1, blocks), jnp.int32),
                shape((1, 1), jnp.int32),
                shape((chunks * 2 * UNROLL, padded, lanes), jnp.bfloat16),
            ),
            in_specs=vmem(1) + smem(1) + hbm(1),
            out_specs=tuple(vmem(4) + smem(3) + hbm(1)),
            scratch_shapes=[
                VMEM((passage_local, padded, feature), jnp.bfloat16),
                VMEM((tiles, feature, lanes), jnp.bfloat16),
                VMEM((passage_local, 128), jnp.int32),
                SMEM((passage_local, 128), jnp.int32),
                VMEM((2 * padded, lanes), jnp.float32),
                VMEM((UNROLL, padded, lanes), jnp.float32),
                VMEM((UNROLL, padded, lanes), jnp.float32),
                VMEM((UNROLL, lanes), jnp.float32),
                VMEM((UNROLL, lanes), jnp.float32),
                VMEM((chunks * 2 * UNROLL, padded, lanes), jnp.bfloat16),
                pltpu.SemaphoreType.DMA,
                pltpu.SemaphoreType.DMA,
                pltpu.SemaphoreType.DMA((chunks,)),
            ],
            name="score",
            compiler_params=params,
        )(arrived, lengths.T, rows)
    )
    all_scores = lax.all_to_all(scores, "grp", split_axis=0, concat_axis=0, tiled=True)
    weight_sums = from_replicas(weight_sum, replicas)

    query_total = query_local * groups * replicas
    grads, multiplier, numerator, weight_sum = pl.pallas_call(
        functools.partial(query_kernel, dims + (query_total, replicas), "grp"),
        out_shape=(
            shape((groups, tokens, feature), jnp.bfloat16),
            shape((tiles, slots, lanes), jnp.float32),
            shape((1, 128), jnp.float32),
            shape((1, 128), jnp.float32),
        ),
        in_specs=vmem(3 + replicas) + smem(3) + hbm(2),
        out_specs=tuple(vmem(4)),
        scratch_shapes=[
            VMEM(rows.shape, jnp.bfloat16),
            VMEM(powers.shape, jnp.bfloat16),
            VMEM((tiles, feature, lanes), jnp.float32),
            pltpu.SemaphoreType.DMA,
            pltpu.SemaphoreType.DMA((chunks,)),
        ],
        name="query_grad",
        compiler_params=params,
    )(arrived, all_scores, summed, *weight_sums, block_row, block_tile, block_count, rows, powers)
    returned = lax.all_to_all(grads, "grp", split_axis=0, concat_axis=0, tiled=True)

    passage_grad = pl.pallas_call(
        functools.partial(passage_kernel, (tokens, per_tile // query_local)),
        out_shape=shape((token_len, passage_local, feature), jnp.bfloat16),
        in_specs=vmem(2) + smem(3) + hbm(1),
        out_specs=pl.BlockSpec(memory_space=VMEM),
        scratch_shapes=[
            VMEM(powers.shape, jnp.bfloat16),
            VMEM(((passage_local + 1) * pitch, feature), jnp.float32),
            VMEM((tiles, lanes, feature), jnp.bfloat16),
            pltpu.SemaphoreType.DMA((chunks,)),
        ],
        name="passage_grad",
        compiler_params=params,
        cost_estimate=pl.CostEstimate(
            flops=2 * limit * padded * lanes * feature,
            bytes_accessed=2 * limit * padded * lanes,
            transcendentals=0,
        ),
    )(arrived, multiplier, block_row, block_tile, block_count, powers)
    numerators = from_replicas(numerator, replicas)

    loss = pair_sums(numerators)[0, 0] / weight_sum[0, 0]
    query_grad = jnp.sum(returned.astype(jnp.float32), axis=0)
    query_grad = query_grad.reshape(query_local, 1, query_len, feature)
    return (loss, query_grad, passage_grad.transpose(1, 0, 2)[:, None])


def solution(mesh):
    return jax.shard_map(
        on_device,
        mesh=mesh,
        in_specs=(
            P("grp", "rep", None, None),
            P("grp", "rep", None, None),
            P("grp", "rep"),
            P("grp", "rep", None),
            P("rep", None),
            P("grp", "rep", None),
            P("grp", "rep"),
        ),
        out_specs=(P(), P("grp", "rep", None, None), P("grp", "rep", None, None)),
        check_vma=False,
    )
```

profile of v0, /device:TPU:0, one launch (start us, length us, event | category | flops | bytes accessed | tf_op | source)
XLA Modules:
  0.0 68.2 jit_solution(9065718409519193537)
XLA Ops:
  0.6 1.6 %pack.1 = bf16[8,80,128]{2,1,0:T(8,128)(2,1)} custom-call(bf16[64,128]{1,0:T(8,128)(2,1)} %bitcast.16, s32[2,1,64]{2,1,0:T(1,128)} %cand_ids.1, s32[1,512]{1,0:T(1,128)} %owner_map.1, f32[2,1,64]{2,1,0:T(1,128)} %teacher.1, f32[1,2]{1,0:T(1,128)} %bitcast.17), custom_call_target="tpu_custom_call" | custom-call | tf_op jit(solution)/shard_map/pack/pallas_call | solution.py:460
  2.2 7.3 %all-to-all-start = ((bf16[8,80,128]{2,1,0:T(8,128)(2,1)}), bf16[8,80,128]{2,1,0:T(8,128)(2,1)S(1)}, u32[]{:S(2)}, u32[]{:S(2)}) async-start(bf16[8,80,128]{2,1,0:T(8,128)(2,1)} %pack.1), calls=%async_computation | async-start | bytes 327680 | tf_op jit(solution)/shard_map/all_to_all | solution.py:469
  9.5 5.4 %prepare.1.passages_hbm.refs_7_ = bf16[64,192,128]{2,1,0:T(8,128)(2,1)} custom-call(bf16[180,64,128]{2,1,0:T(8,128)(2,1)} %bitcast.13), custom_call_target="tpu_custom_call" | custom-call | tf_op jit(solution)/shard_map/prepare/pallas_call | solution.py:472
  14.9 2.2 %all-to-all-done.arrived = bf16[8,80,128]{2,1,0:T(8,128)(2,1)S(1)} async-done(((bf16[8,80,128]{2,1,0:T(8,128)(2,1)}), bf16[8,80,128]{2,1,0:T(8,128)(2,1)S(1)}, u32[]{:S(2)}, u32[]{:S(2)}) %all-to-all-start) | async-done | bytes 163872 | tf_op jit(solution)/shard_map/all_to_all | solution.py:469
  17.1 0.0 copy-start
  17.1 0.7 copy-done
  17.8 12.1 %score.1 = (f32[8,16,128]{2,1,0:T(8,128)}, f32[4,72,128]{2,1,0:T(8,128)}, f32[4,72,128]{2,1,0:T(8,128)}, f32[1,128]{1,0:T(1,128)}, s32[1,280]{1,0:T(1,128)}, /*i...) custom-call(bf16[8,80,128]{2,1,0:T(8,128)(2,1)} %copy-done, s32[1,64]{1,0:T(1,128)} %bitcast.19, ...), custom_call_target="tpu_custom_call" | custom-call | tf_op jit(solution)/shard_map/score/pallas_call | solution.py:485
  29.9 3.4 %all-to-all-start.1 = ((f32[8,16,128]{2,1,0:T(8,128)}), f32[8,16,128]{2,1,0:T(8,128)S(1)}, u32[]{:S(2)}, u32[]{:S(2)}) async-start(f32[8,16,128]{2,1,0:T(8,128)} %get-tuple-element.14), calls=%async_computation.1 | async-start | bytes 131072 | tf_op jit(solution)/shard_map/all_to_all | solution.py:518
  33.3 0.1 collective-permute-start.2
  33.3 0.1 collective-permute-start.1
  33.4 1.8 %collective-permute-start = (f32[1,128]{1,0:T(1,128)}, f32[1,128]{1,0:T(1,128)S(1)}, u32[]{:S(2)}, u32[]{:S(2)}) collective-permute-start(f32[1,128]{1,0:T(1,128)} %get-tuple-element.16.refs_0_), channel_id=1, source_target_pairs={{0,1},{1,0},{2,3},{3,2},{4,5},{5,4},{6,7},{7,6},{8,9},{9,8},{10,11... | collective-permute-start | bytes 1544 | tf_op jit(solution)/shard_map/ppermute | solution.py:430
  35.2 1.3 %collective-permute-done.2.refs_3_ = f32[1,128]{1,0:T(1,128)S(1)} collective-permute-done((f32[1,128]{1,0:T(1,128)}, f32[1,128]{1,0:T(1,128)S(1)}, u32[]{:S(2)}, u32[]{:S(2)}) %collective-permute-start.2) | collective-permute-done | bytes 544 | tf_op jit(solution)/shard_map/ppermute | solution.py:430
  36.5 0.0 copy-start.2
  36.5 0.7 collective-permute-done.1.refs_2_
  37.1 0.0 copy-start.3
  37.1 0.0 collective-permute-done.refs_1_
  37.1 0.0 copy-start.4
  37.1 3.0 %all-to-all-done.1.scores = f32[8,16,128]{2,1,0:T(8,128)S(1)} async-done(((f32[8,16,128]{2,1,0:T(8,128)}), f32[8,16,128]{2,1,0:T(8,128)S(1)}, u32[]{:S(2)}, u32[]{:S(2)}) %all-to-all-start.1) | async-done | bytes 65568 | tf_op jit(solution)/shard_map/all_to_all | solution.py:518
  40.1 0.0 copy-start.1
  40.1 0.0 copy-done.2
  40.1 0.0 copy-done.3
  40.1 0.0 copy-done.4
  40.1 0.6 copy-done.1
  40.7 10.2 %query_grad.1 = (bf16[8,64,128]{2,1,0:T(8,128)(2,1)}, f32[4,72,128]{2,1,0:T(8,128)}, f32[1,128]{1,0:T(1,128)}, f32[1,128]{1,0:T(1,128)}) custom-call(bf16[8,80,128]{2,1,0:T(8,128)(2,1)} %copy-done, f32[8,16,128]{2,1,0:T(8,128)} %copy-done.1, f32[4,72,128]{2,1,0:T(8,128)} %get-tuple-element.15.summed, f32[1,128]{1,0:T(1,128)} %get-tuple-element.16.refs_0_, ...), custom_call_target="tpu_custom_call" | custom-call | tf_op jit(solution)/shard_map/query_grad/pallas_call | solution.py:522
  50.9 0.1 collective-permute-start.5
  51.0 0.1 collective-permute-start.4
  51.1 1.8 %collective-permute-start.3 = (f32[1,128]{1,0:T(1,128)}, f32[1,128]{1,0:T(1,128)S(1)}, u32[]{:S(2)}, u32[]{:S(2)}) collective-permute-start(f32[1,128]{1,0:T(1,128)} %get-tuple-element.21), channel_id=1, source_target_pairs={{0,1},{1,0},{2,3},{3,2},{4,5},{5,4},{6,7},{7,6},{8,9},{9,8},{10,11... | collective-permute-start | bytes 1544 | tf_op jit(solution)/shard_map/ppermute | solution.py:430
  52.9 3.4 %all-to-all-start.2 = ((bf16[8,64,128]{2,1,0:T(8,128)(2,1)}), bf16[8,64,128]{2,1,0:T(8,128)(2,1)S(1)}, u32[]{:S(2)}, u32[]{:S(2)}) async-start(bf16[8,64,128]{2,1,0:T(8,128)(2,1)} %get-tuple-element.23), calls=%async_computation.2 | async-start | bytes 262144 | tf_op jit(solution)/shard_map/all_to_all | solution.py:542
  56.3 0.0 copy-start.5
  56.3 0.0 copy-start.6
  56.3 10.0 %passage_grad.1 = bf16[180,64,128]{2,1,0:T(8,128)(2,1)} custom-call(bf16[8,80,128]{2,1,0:T(8,128)(2,1)} %copy-done, f32[4,72,128]{2,1,0:T(8,128)} %get-tuple-element.24.multiplier, s32[1,280]{1,0:T(1,128)} %get-tuple-element.17.refs_4_.block_row, s32[1,280]{1,0:T(1,128)} %get-tuple-element.18.refs_5_.block_tile, ...), custom_call_target="tpu_custom_call" | custom-call | flops 1610612736 | bytes 12582912 | tf_op jit(solution)/shard_map/passage_grad/pallas_call | solution.py:544
  66.3 0.0 collective-permute-done.5
  66.3 0.0 collective-permute-done.4
  66.3 0.0 collective-permute-done.3
  66.3 0.0 copy-done.5
  66.4 0.0 copy-done.6
  66.4 0.0 all-to-all-done.2
  66.5 0.6 convert_reduce_fusion
  (1 shorter events, 0.0 us)
Async XLA Ops:
  2.2 14.9 %all-to-all-start = ((bf16[8,80,128]{2,1,0:T(8,128)(2,1)}), bf16[8,80,128]{2,1,0:T(8,128)(2,1)S(1)}, u32[]{:S(2)}, u32[]{:S(2)}) async-start(bf16[8,80,128]{2,1,0:T(8,128)(2,1)} %pack.1), calls=%async_computation | async-start | bytes 327680 | tf_op jit(solution)/shard_map/all_to_all | solution.py:469
  17.1 0.7 copy-start
  29.9 10.2 %all-to-all-start.1 = ((f32[8,16,128]{2,1,0:T(8,128)}), f32[8,16,128]{2,1,0:T(8,128)S(1)}, u32[]{:S(2)}, u32[]{:S(2)}) async-start(f32[8,16,128]{2,1,0:T(8,128)} %get-tuple-element.14), calls=%async_computation.1 | async-start | bytes 131072 | tf_op jit(solution)/shard_map/all_to_all | solution.py:518
  33.3 3.2 %collective-permute-start.2 = (f32[1,128]{1,0:T(1,128)}, f32[1,128]{1,0:T(1,128)S(1)}, u32[]{:S(2)}, u32[]{:S(2)}) collective-permute-start(f32[1,128]{1,0:T(1,128)} %get-tuple-element.16.refs_0_), channel_id=1, source_target_pairs={{0,3},{1,2},{2,1},{3,0},{4,7},{5,6},{6,5},{7,4},{8,11},{9,10},{10,... | collective-permute-start | bytes 1544 | tf_op jit(solution)/shard_map/ppermute | solution.py:430
  33.3 3.8 %collective-permute-start.1 = (f32[1,128]{1,0:T(1,128)}, f32[1,128]{1,0:T(1,128)S(1)}, u32[]{:S(2)}, u32[]{:S(2)}) collective-permute-start(f32[1,128]{1,0:T(1,128)} %get-tuple-element.16.refs_0_), channel_id=1, source_target_pairs={{0,2},{1,3},{2,0},{3,1},{4,6},{5,7},{6,4},{7,5},{8,10},{9,11},{10,... | collective-permute-start | bytes 1544 | tf_op jit(solution)/shard_map/ppermute | solution.py:430
  33.4 3.7 %collective-permute-start = (f32[1,128]{1,0:T(1,128)}, f32[1,128]{1,0:T(1,128)S(1)}, u32[]{:S(2)}, u32[]{:S(2)}) collective-permute-start(f32[1,128]{1,0:T(1,128)} %get-tuple-element.16.refs_0_), channel_id=1, source_target_pairs={{0,1},{1,0},{2,3},{3,2},{4,5},{5,4},{6,7},{7,6},{8,9},{9,8},{10,11... | collective-permute-start | bytes 1544 | tf_op jit(solution)/shard_map/ppermute | solution.py:430
  36.5 3.7 %copy-start.2 = (f32[1,128]{1,0:T(1,128)}, f32[1,128]{1,0:T(1,128)S(1)}, u32[]{:S(2)}) copy-start(f32[1,128]{1,0:T(1,128)S(1)} %collective-permute-done.2.refs_3_) | copy-start | bytes 1540
  37.1 3.0 %copy-start.3 = (f32[1,128]{1,0:T(1,128)}, f32[1,128]{1,0:T(1,128)S(1)}, u32[]{:S(2)}) copy-start(f32[1,128]{1,0:T(1,128)S(1)} %collective-permute-done.1.refs_2_) | copy-start | bytes 1540
  37.1 3.0 %copy-start.4 = (f32[1,128]{1,0:T(1,128)}, f32[1,128]{1,0:T(1,128)S(1)}, u32[]{:S(2)}) copy-start(f32[1,128]{1,0:T(1,128)S(1)} %collective-permute-done.refs_1_) | copy-start | bytes 1540
  40.1 0.6 copy-start.1
  50.9 15.4 %collective-permute-start.5 = (f32[1,128]{1,0:T(1,128)}, f32[1,128]{1,0:T(1,128)S(1)}, u32[]{:S(2)}, u32[]{:S(2)}) collective-permute-start(f32[1,128]{1,0:T(1,128)} %get-tuple-element.21), channel_id=1, source_target_pairs={{0,3},{1,2},{2,1},{3,0},{4,7},{5,6},{6,5},{7,4},{8,11},{9,10},{10,... | collective-permute-start | bytes 1544 | tf_op jit(solution)/shard_map/ppermute | solution.py:430
  51.0 15.3 %collective-permute-start.4 = (f32[1,128]{1,0:T(1,128)}, f32[1,128]{1,0:T(1,128)S(1)}, u32[]{:S(2)}, u32[]{:S(2)}) collective-permute-start(f32[1,128]{1,0:T(1,128)} %get-tuple-element.21), channel_id=1, source_target_pairs={{0,2},{1,3},{2,0},{3,1},{4,6},{5,7},{6,4},{7,5},{8,10},{9,11},{10,... | collective-permute-start | bytes 1544 | tf_op jit(solution)/shard_map/ppermute | solution.py:430
  51.1 15.2 %collective-permute-start.3 = (f32[1,128]{1,0:T(1,128)}, f32[1,128]{1,0:T(1,128)S(1)}, u32[]{:S(2)}, u32[]{:S(2)}) collective-permute-start(f32[1,128]{1,0:T(1,128)} %get-tuple-element.21), channel_id=1, source_target_pairs={{0,1},{1,0},{2,3},{3,2},{4,5},{5,4},{6,7},{7,6},{8,9},{9,8},{10,11... | collective-permute-start | bytes 1544 | tf_op jit(solution)/shard_map/ppermute | solution.py:430
  52.9 13.6 %all-to-all-start.2 = ((bf16[8,64,128]{2,1,0:T(8,128)(2,1)}), bf16[8,64,128]{2,1,0:T(8,128)(2,1)S(1)}, u32[]{:S(2)}, u32[]{:S(2)}) async-start(bf16[8,64,128]{2,1,0:T(8,128)(2,1)} %get-tuple-element.23), calls=%async_computation.2 | async-start | bytes 262144 | tf_op jit(solution)/shard_map/all_to_all | solution.py:542
  56.3 10.1 %copy-start.5 = (f32[1,128]{1,0:T(1,128)S(1)}, f32[1,128]{1,0:T(1,128)}, u32[]{:S(2)}) copy-start(f32[1,128]{1,0:T(1,128)} %get-tuple-element.21) | copy-start | bytes 1540
  56.3 10.1 %copy-start.6 = (f32[1,128]{1,0:T(1,128)S(1)}, f32[1,128]{1,0:T(1,128)}, u32[]{:S(2)}) copy-start(f32[1,128]{1,0:T(1,128)} %get-tuple-element.22) | copy-start | bytes 1540
where the time goes:
time: 67.6 us; the launch traced here: 68.2 us
  Pallas kernels  39.3 us (58%)
  starting transfers between devices  17.9 us (26%)
  waiting for transfers between devices  7.12 us (11%)
  between operations  1.99 us (3%)
  local copies, waits for them, and re-layouts  1.29 us (2%)
    pallas_call x1, Pallas kernels, on_device(): pl.pallas_call(functools.partial(score_kernel, dims, 'grp'), out_shape=(s...  12.1 us
    pallas_call x1, Pallas kernels, on_device(): pl.pallas_call(functools.partial(query_kernel, dims + (query_total, repli...  10.2 us
    pallas_call x1, Pallas kernels, on_device(): pl.pallas_call(functools.partial(passage_kernel, (tokens, per_tile // que...  10 us
    all_to_all x1, starting transfers between devices, on_device(): lax.all_to_all(share, 'grp', split_axis=0, concat_axis=0, tiled=True)  7.31 us
    pallas_call x1, Pallas kernels, on_device(): pl.pallas_call(prepare_kernel, grid=(passage_local // chunk,), out_shape=...  5.36 us
    ppermute x6, starting transfers between devices, from_replicas(): return [values] + [lax.ppermute(values, 'rep', ring) for ring in rings]  3.82 us
    all_to_all x1, starting transfers between devices, on_device(): lax.all_to_all(grads, 'grp', split_axis=0, concat_axis=0, tiled=True)  3.37 us
    all_to_all x1, starting transfers between devices, on_device(): lax.all_to_all(scores, 'grp', split_axis=0, concat_axis=0, tiled=True)  3.36 us
  transfers between devices with their start and end apart: 9, of which 4 were waited for; matrix products, arithmetic and copies ran while one was open for 0% of the time, Pallas kernels for 23%

commit v1 on v0

--- a/solution.py
+++ b/solution.py
@@ -8,12 +8,15 @@
 from jax.experimental.pallas import tpu as pltpu
 from jax.sharding import PartitionSpec as P
 
+
 TEMPER = 0.05
 LOG2E = math.log2(math.e)
 MASKED = -1e30
 KINDS = 8
 UNROLL = 8
 SPREAD = 4
+STORE = 5
+PIECES = 4
 HIGHEST = lax.Precision.HIGHEST
 VMEM = pltpu.VMEM
 SMEM = pltpu.SMEM
@@ -93,21 +96,34 @@
         rows_out[p] = gathered[p * pitch : p * pitch + padded, :].astype(jnp.bfloat16)
 
 
-def list_blocks(flags_scalar, block_row, block_tile, block_count, passage_count, tiles):
-    def list_passage(p, count):
-        for tile in range(tiles):
-            block_row[0, count] = p
-            block_tile[0, count] = tile
-            count = count + flags_scalar[p, tile]
+def list_blocks(flags_scalar, block_code, block_count, passage_count, tiles):
+    base = code_base(tiles)
+    ahead = math.gcd(passage_count, 4)
+
+    def list_passages(step, count):
+        for inner in range(ahead):
+            p = step * ahead + inner
+            for tile in range(tiles):
+                block_code[0, count] = p * base + tile
+                count = count + flags_scalar[p, tile]
         return count
 
-    count = lax.fori_loop(0, passage_count, list_passage, jnp.int32(0))
+    count = lax.fori_loop(0, passage_count // ahead, list_passages, jnp.int32(0))
     for extra in range(3 * UNROLL):
-        block_row[0, count + extra] = passage_count
-        block_tile[0, count + extra] = 0
+        block_code[0, count + extra] = passage_count * base
     steps = (count + 2 * UNROLL - 1) // (2 * UNROLL)
     block_count[0, 0] = steps
     return steps
+
+
+def code_base(tiles):
+    return 1 << (tiles - 1).bit_length()
+
+
+def decode(block_code, block, tiles):
+    code = block_code[0, block]
+    base = code_base(tiles)
+    return code >> (base.bit_length() - 1), code & (base - 1)
 
 
 def score_kernel(
@@ -115,15 +131,40 @@
     axis,
     arrived,
     lengths,
+    *refs,
+):
+    tokens, query_local, candidates, per_tile, replicas = dims
+    weights, refs = refs[:replicas], refs[replicas:]
+    passages_hbm, scores_out, summed, block_code, block_count, powers_hbm, *scratch = refs
+    score_body(
+        (tokens, query_local, candidates, per_tile),
+        lax.axis_index(axis),
+        arrived,
+        lengths,
+        pair_sums([one[...] for one in weights]),
+        passages_hbm,
+        scores_out,
+        summed,
+        block_code,
+        block_count,
+        powers_hbm,
+        *scratch,
+    )
+
+
+def score_body(
+    dims,
+    me,
+    arrived,
+    lengths,
+    weights,
     passages_hbm,
     scores_out,
-    highest,
     summed,
-    weight_sum,
-    block_row,
-    block_tile,
+    block_code,
     block_count,
     powers_hbm,
+    highest,
     passages,
     turned,
     flags,
@@ -140,9 +181,8 @@
 ):
     tokens, query_local, candidates, per_tile = dims
     groups = arrived.shape[0]
-    passage_count, padded, feature = passages.shape
+    passage_count, padded, _ = passages.shape
     tiles, _, lanes = highest.shape
-    me = lax.axis_index(axis)
     groups_per_tile = per_tile // query_local
     fetch_rows = pltpu.make_async_copy(passages_hbm, passages, rows_done)
     fetch_rows.start()
@@ -162,13 +202,6 @@
     to_scalar = pltpu.make_async_copy(flags, flags_scalar, flags_done)
     to_scalar.start()
 
-    total = jnp.zeros((1, 1), jnp.float32)
-    for g in range(groups):
-        for q in range(query_local):
-            for part in range(5, 8):
-                at = tokens + part * query_local + q
-                total = total + arrived[g, at : at + 1, 0:1].astype(jnp.float32)
-    weight_sum[...] = jnp.broadcast_to(total, weight_sum.shape)
     for tile in range(tiles):
         parts = [
             arrived[g, 0:tokens, :]
@@ -180,15 +213,15 @@
     summed[...] = jnp.ones_like(summed)
     penalty[...] = jnp.where(iota(penalty.shape, 0) < padded, 0.0, MASKED)
     to_scalar.wait()
-    steps = list_blocks(flags_scalar, block_row, block_tile, block_count, passage_count, tiles)
+    steps = list_blocks(flags_scalar, block_code, block_count, passage_count, tiles)
     fetch_rows.wait()
 
     factor = LOG2E / TEMPER
 
     def multiply(first, into, tops):
         for u in range(UNROLL):
-            p = jnp.minimum(block_row[0, first + u], passage_count - 1)
-            tile = block_tile[0, first + u]
+            slot, tile = decode(block_code, first + u, tiles)
+            p = jnp.minimum(slot, passage_count - 1)
             products = jnp.dot(passages[p], turned[tile], preferred_element_type=jnp.float32)
             products = products + penalty[pl.ds(padded - lengths[0, p], padded), :]
             into[u] = products
@@ -196,8 +229,7 @@
 
     def soften(first, held, tops):
         for u in range(UNROLL):
-            slot = block_row[0, first + u]
-            tile = block_tile[0, first + u]
+            slot, tile = decode(block_code, first + u, tiles)
             top = tops[u : u + 1, :]
             raised = jnp.exp2((held[u] - top) * factor)
             powers[first + u] = raised.astype(jnp.bfloat16)
@@ -224,7 +256,8 @@
     query_len = lanes // per_tile
     member = iota((lanes, 128), 0) // query_len == iota((lanes, 128), 1)
     member = member.astype(jnp.float32)
-    scores_out[0] = jnp.zeros(scores_out.shape[1:], jnp.float32)
+    weight_part = jnp.sum(weights, axis=1, keepdims=True)
+    scores_out[0] = jnp.broadcast_to(weight_part, scores_out.shape[1:])
     for tile in range(tiles):
         matched = highest[tile, 0:passage_count, :] + TEMPER * jnp.log(
             summed[tile, 0:passage_count, :]
@@ -253,15 +286,30 @@
     return values[0]
 
 
-def query_kernel(dims, axis, arrived, scores, summed, *refs):
-    tokens, query_local, candidates, per_tile, query_total, replicas = dims
-    weight_sums, refs = refs[:replicas], refs[replicas:]
-    block_row, block_tile, block_count, passages_hbm, powers_hbm = refs[:5]
-    grads_out, multiplier, numerator_out, weight_sum_out = refs[5:9]
-    passages, powers, sums, rows_done, powers_done = refs[9:]
+def query_kernel(
+    dims,
+    axis,
+    arrived,
+    scores,
+    summed,
+    block_code,
+    block_count,
+    passages_hbm,
+    powers_hbm,
+    grads_out,
+    multiplier,
+    numerator_out,
+    weight_sum_out,
+    passages,
+    powers,
+    sums,
+    rows_done,
+    powers_done,
+):
+    tokens, query_local, candidates, per_tile, query_total = dims
     groups = arrived.shape[0]
     tiles, slots, lanes = summed.shape
-    passage_count, padded, _ = passages.shape
+    passage_count, _, _ = passages.shape
     groups_per_tile = per_tile // query_local
     queries_all = tiles * per_tile
     query_len = lanes // per_tile
@@ -305,9 +353,9 @@
     spread = jnp.sum(weight * teacher_prob * (log_teacher - log_student), axis=1, keepdims=True)
     numerator = jnp.sum(spread, axis=0, keepdims=True)
     numerator_out[...] = jnp.broadcast_to(numerator, numerator_out.shape)
-    weight_sum = pair_sums([one[...] for one in weight_sums])
-    weight_sum_out[...] = weight_sum
-    scale = query_total / weight_sum[0:1, 0:1]
+    weight_sum = got[0:1, candidates : candidates + 1]
+    weight_sum_out[...] = jnp.broadcast_to(weight_sum, weight_sum_out.shape)
+    scale = query_total / weight_sum
     grad = (weight * scale) * (jnp.exp(log_student) - teacher_prob)
 
     passage_index = iota((passage_count, candidates), 0)
@@ -332,8 +380,7 @@
         chunk_copy(s).wait()
         for u in range(2 * UNROLL):
             b = s * 2 * UNROLL + u
-            slot = block_row[0, b]
-            tile = block_tile[0, b]
+            slot, tile = decode(block_code, b, tiles)
             p = jnp.minimum(slot, passage_count - 1)
             part = powers[b].astype(jnp.float32) * multiplier[tile, pl.ds(slot, 1), :]
             part = part.astype(jnp.bfloat16)
@@ -354,15 +401,16 @@
     dims,
     arrived,
     multiplier,
-    block_row,
-    block_tile,
+    block_code,
     block_count,
     powers_hbm,
+    out_hbm,
     out,
     powers,
     sums,
     queries_all,
     powers_done,
+    out_done,
 ):
     tokens, per_tile_groups = dims
     token_len, passage_count, feature = out.shape
@@ -395,10 +443,9 @@
         chunk_copy(s).wait()
         for u in range(2 * UNROLL):
             b = s * 2 * UNROLL + u
-            slot = block_row[0, b]
-            tile = block_tile[0, b]
+            slot, tile = decode(block_code, b, tiles)
             part = powers[b].astype(jnp.float32) * multiplier[tile, pl.ds(slot, 1), :]
-            at = pl.ds(pl.multiple_of(slot * pitch, 8), padded)
+            at = pl.ds(slot * pitch, padded)
             sums[at, :] += jnp.dot(
                 part.astype(jnp.bfloat16), queries_all[tile], preferred_element_type=jnp.float32
             )
@@ -406,15 +453,28 @@
 
     lax.fori_loop(0, steps, step, 0)
 
-    def store(j, carry):
-        for u in range(SPREAD):
-            at = j * SPREAD + u
+    pieces = out_done.shape[0]
+    piece = token_len // pieces
+    copies = []
+    for k in range(pieces):
+        first = k * piece
+        last = token_len if k == pieces - 1 else first + piece
+
+        def store(j, carry, first=first):
+            for u in range(STORE):
+                at = first + j * STORE + u
+                out[at] = sums[pl.ds(at, passage_count, stride=pitch), :].astype(out.dtype)
+            return carry
+
+        whole = (last - first) // STORE
+        lax.fori_loop(0, whole, store, 0)
+        for at in range(first + whole * STORE, last):
             out[at] = sums[pl.ds(at, passage_count, stride=pitch), :].astype(out.dtype)
-        return carry
-
-    lax.fori_loop(0, token_len // SPREAD, store, 0)
-    for j in range(token_len - token_len % SPREAD, token_len):
-        out[j] = sums[pl.ds(j, passage_count, stride=pitch), :].astype(out.dtype)
+        rows = pl.ds(first, last - first)
+        copies.append(pltpu.make_async_copy(out.at[rows], out_hbm.at[rows], out_done.at[k]))
+        copies[-1].start()
+    for copy in copies:
+        copy.wait()
 
 
 def vmem(count):
@@ -445,7 +505,7 @@
     per_tile = lanes // query_len
     tiles = groups * tokens // lanes
     padded = round_up(token_len, 16)
-    pitch = round_up(padded, 16) + 8
+    pitch = padded + 9
     ref_count = query_local * candidates
     capacity = groups * (2 * ref_count // groups)
     limit = min(passage_local * tiles, capacity)
@@ -455,7 +515,8 @@
     slots = round_up(passage_local + 1, 8)
     score_rows = round_up(groups * query_local, 8)
     shape = jax.ShapeDtypeStruct
-    params = pltpu.CompilerParams(vmem_limit_bytes=62 * 2**20)
+    alone = pltpu.CompilerParams(vmem_limit_bytes=62 * 2**20)
+    params = pltpu.CompilerParams(vmem_limit_bytes=52 * 2**20)
 
     share = pl.pallas_call(
         functools.partial(pack_kernel, passage_local),
@@ -464,9 +525,11 @@
         out_specs=pl.BlockSpec(memory_space=VMEM),
         scratch_shapes=[VMEM((aux_rows, feature), jnp.float32)],
         name="pack",
-        compiler_params=params,
+        compiler_params=alone,
     )(queries.reshape(tokens, feature), cand_ids, owner_map, teacher, weights.T)
     arrived = lax.all_to_all(share, "grp", split_axis=0, concat_axis=0, tiled=True)
+
+    replica_weights = from_replicas(weights.T, replicas)
 
     chunk = math.gcd(passage_local, 16)
     rows = pl.pallas_call(
@@ -481,22 +544,20 @@
     )(passages[:, 0].transpose(1, 0, 2))
 
     dims = (tokens, query_local, candidates, per_tile)
-    scores, highest, summed, weight_sum, block_row, block_tile, block_count, powers = (
+    scores, summed, block_code, block_count, powers = (
         pl.pallas_call(
-            functools.partial(score_kernel, dims, "grp"),
+            functools.partial(score_kernel, dims + (replicas,), "grp"),
             out_shape=(
                 shape((groups, score_rows, 128), jnp.float32),
                 shape((tiles, slots, lanes), jnp.float32),
-                shape((tiles, slots, lanes), jnp.float32),
-                shape((1, 128), jnp.float32),
-                shape((1, blocks), jnp.int32),
                 shape((1, blocks), jnp.int32),
                 shape((1, 1), jnp.int32),
                 shape((chunks * 2 * UNROLL, padded, lanes), jnp.bfloat16),
             ),
-            in_specs=vmem(1) + smem(1) + hbm(1),
-            out_specs=tuple(vmem(4) + smem(3) + hbm(1)),
+            in_specs=vmem(1) + smem(1) + vmem(replicas) + hbm(1),
+            out_specs=tuple(vmem(2) + smem(2) + hbm(1)),
             scratch_shapes=[
+                VMEM((tiles, slots, lanes), jnp.float32),
                 VMEM((passage_local, padded, feature), jnp.bfloat16),
                 VMEM((tiles, feature, lanes), jnp.bfloat16),
                 VMEM((passage_local, 128), jnp.int32),
@@ -513,21 +574,20 @@
             ],
             name="score",
             compiler_params=params,
-        )(arrived, lengths.T, rows)
+        )(arrived, lengths.T, *replica_weights, rows)
     )
     all_scores = lax.all_to_all(scores, "grp", split_axis=0, concat_axis=0, tiled=True)
-    weight_sums = from_replicas(weight_sum, replicas)
 
     query_total = query_local * groups * replicas
     grads, multiplier, numerator, weight_sum = pl.pallas_call(
-        functools.partial(query_kernel, dims + (query_total, replicas), "grp"),
+        functools.partial(query_kernel, dims + (query_total,), "grp"),
         out_shape=(
             shape((groups, tokens, feature), jnp.bfloat16),
             shape((tiles, slots, lanes), jnp.float32),
             shape((1, 128), jnp.float32),
             shape((1, 128), jnp.float32),
         ),
-        in_specs=vmem(3 + replicas) + smem(3) + hbm(2),
+        in_specs=vmem(3) + smem(2) + hbm(2),
         out_specs=tuple(vmem(4)),
         scratch_shapes=[
             VMEM(rows.shape, jnp.bfloat16),
@@ -538,19 +598,21 @@
         ],
         name="query_grad",
         compiler_params=params,
-    )(arrived, all_scores, summed, *weight_sums, block_row, block_tile, block_count, rows, powers)
+    )(arrived, all_scores, summed, block_code, block_count, rows, powers)
     returned = lax.all_to_all(grads, "grp", split_axis=0, concat_axis=0, tiled=True)
 
     passage_grad = pl.pallas_call(
         functools.partial(passage_kernel, (tokens, per_tile // query_local)),
         out_shape=shape((token_len, passage_local, feature), jnp.bfloat16),
-        in_specs=vmem(2) + smem(3) + hbm(1),
-        out_specs=pl.BlockSpec(memory_space=VMEM),
+        in_specs=vmem(2) + smem(2) + hbm(1),
+        out_specs=pl.BlockSpec(memory_space=pltpu.HBM),
         scratch_shapes=[
+            VMEM((token_len, passage_local, feature), jnp.bfloat16),
             VMEM(powers.shape, jnp.bfloat16),
             VMEM(((passage_local + 1) * pitch, feature), jnp.float32),
             VMEM((tiles, lanes, feature), jnp.bfloat16),
             pltpu.SemaphoreType.DMA((chunks,)),
+            pltpu.SemaphoreType.DMA((PIECES,)),
         ],
         name="passage_grad",
         compiler_params=params,
@@ -559,7 +621,7 @@
             bytes_accessed=2 * limit * padded * lanes,
             transcendentals=0,
         ),
-    )(arrived, multiplier, block_row, block_tile, block_count, powers)
+    )(arrived, multiplier, block_code, block_count, powers)
     numerators = from_replicas(numerator, replicas)
 
     loss = pair_sums(numerators)[0, 0] / weight_sum[0, 0]

time: 67.6 us -> 63.5 us (0.939); the launches traced: 68.2 us -> 63 us
  blocking collectives: 0 us -> 13 us
  Pallas kernels: 39.3 us -> 30 us
  waiting for transfers between devices: 7.12 us -> 1.64 us
  starting transfers between devices: 17.9 us -> 15.9 us
  local copies, waits for them, and re-layouts: 1.29 us -> 0.01 us
    all_to_all x0 -> x1, blocking collectives: none -> 13 us  [on_device(): lax.all_to_all(scores, 'grp', split_axis=0, concat_axis=0, tiled=True)]
    pallas_call x2, Pallas kernels: 22.3 us -> 16.8 us  [the longest x1 8.5 us: on_device(): pl.pallas_call(functools.partial(query_kernel, dims + (query_total,), 'gr...]
    pallas_call x1, Pallas kernels: 10 us -> 6.62 us  [on_device(): pl.pallas_call(functools.partial(passage_kernel, (tokens, per_tile // que...]
    all_to_all x1 -> x0, starting transfers between devices: 3.36 us -> none  [on_device(): lax.all_to_all(scores, 'grp', split_axis=0, concat_axis=0, tiled=True)]
    all_to_all x1 -> x0, waiting for transfers between devices: 2.99 us -> none  [on_device(): lax.all_to_all(scores, 'grp', split_axis=0, concat_axis=0, tiled=True)]
    ppermute x6, waiting for transfers between devices: 1.93 us -> 0.02 us  [from_replicas(): return [values] + [lax.ppermute(values, 'rep', ring) for ring in rings]]
    all_to_all x1, waiting for transfers between devices: 2.21 us -> 0.75 us  [on_device(): lax.all_to_all(share, 'grp', split_axis=0, concat_axis=0, tiled=True)]
    unnamed x14 -> x4, local copies, waits for them, and re-layouts: 1.29 us -> 0.01 us
  transfers between devices with their start and end apart: 9 -> 8, of which waited for: 4 -> 2; matrix products, arithmetic and copies ran while one was open for 0% -> 0% of each run, Pallas kernels for 23% -> 18%
where the time goes in v1:
time: 63.5 us; the launch traced here: 63 us
  Pallas kernels  30 us (47%)
  starting transfers between devices  15.9 us (25%)
  blocking collectives  13 us (20%)
  between operations  1.91 us (3%)
  waiting for transfers between devices  1.64 us (3%)
  other arithmetic  0.64 us (1%)
    all_to_all x1, blocking collectives, on_device(): lax.all_to_all(scores, 'grp', split_axis=0, concat_axis=0, tiled=True)  13 us
    pallas_call x1, Pallas kernels, on_device(): pl.pallas_call(functools.partial(query_kernel, dims + (query_total,), 'gr...  8.5 us
    pallas_call x1, Pallas kernels, on_device(): pl.pallas_call(functools.partial(score_kernel, dims + (replicas,), 'grp')...  8.3 us
    all_to_all x1, starting transfers between devices, on_device(): lax.all_to_all(share, 'grp', split_axis=0, concat_axis=0, tiled=True)  7.44 us
    pallas_call x1, Pallas kernels, on_device(): pl.pallas_call(functools.partial(passage_kernel, (tokens, per_tile // que...  6.62 us
    pallas_call x1, Pallas kernels, on_device(): pl.pallas_call(prepare_kernel, grid=(passage_local // chunk,), out_shape=...  4.94 us
    all_to_all x1, starting transfers between devices, on_device(): lax.all_to_all(grads, 'grp', split_axis=0, concat_axis=0, tiled=True)  4.36 us
    ppermute x6, starting transfers between devices, from_replicas(): return [values] + [lax.ppermute(values, 'rep', ring) for ring in rings]  4.08 us
  transfers between devices with their start and end apart: 8, of which 2 were waited for; matrix products, arithmetic and copies ran while one was open for 0% of the time, Pallas kernels for 18%

profile of v1, /device:TPU:0, one launch (start us, length us, event | category | flops | bytes accessed | tf_op | source)
XLA Modules:
  0.0 63.0 jit_solution(11036559789820294939)
XLA Ops:
  0.6 1.6 %pack.1 = bf16[8,80,128]{2,1,0:T(8,128)(2,1)} custom-call(bf16[64,128]{1,0:T(8,128)(2,1)} %bitcast.23, s32[2,1,64]{2,1,0:T(1,128)} %cand_ids.1, s32[1,512]{1,0:T(1,128)} %owner_map.1, f32[2,1,64]{2,1,0:T(1,128)} %teacher.1, f32[1,2]{1,0:T(1,128)} %bitcast.13), custom_call_target="tpu_custom_call" | custom-call | tf_op jit(solution)/shard_map/pack/pallas_call | solution.py:521
  2.2 0.0 copy-start
  2.2 0.0 copy-start.1
  2.2 7.4 %all-to-all-start = ((bf16[8,80,128]{2,1,0:T(8,128)(2,1)}), bf16[8,80,128]{2,1,0:T(8,128)(2,1)S(1)}, u32[]{:S(2)}, u32[]{:S(2)}) async-start(bf16[8,80,128]{2,1,0:T(8,128)(2,1)} %pack.1), calls=%async_computation | async-start | bytes 327680 | tf_op jit(solution)/shard_map/all_to_all | solution.py:530
  9.7 0.7 %collective-permute-start.2 = (f32[1,2]{1,0:T(1,128)}, f32[1,2]{1,0:T(1,128)S(1)}, u32[]{:S(2)}, u32[]{:S(2)}) collective-permute-start(f32[1,2]{1,0:T(1,128)} %bitcast.14), channel_id=1, source_target_pairs={{0,3},{1,2},{2,1},{3,0},{4,7},{5,6},{6,5},{7,4},{8,11},{9,10},{10,... | collective-permute-start | bytes 32 | tf_op jit(solution)/shard_map/ppermute | solution.py:490
  10.3 0.9 %collective-permute-start.1 = (f32[1,2]{1,0:T(1,128)}, f32[1,2]{1,0:T(1,128)S(1)}, u32[]{:S(2)}, u32[]{:S(2)}) collective-permute-start(f32[1,2]{1,0:T(1,128)} %bitcast.15), channel_id=1, source_target_pairs={{0,2},{1,3},{2,0},{3,1},{4,6},{5,7},{6,4},{7,5},{8,10},{9,11},{10,... | collective-permute-start | bytes 32 | tf_op jit(solution)/shard_map/ppermute | solution.py:490
  11.3 0.3 collective-permute-start
  11.5 4.9 %prepare.1.refs_4_.passages_hbm = bf16[64,192,128]{2,1,0:T(8,128)(2,1)} custom-call(bf16[180,64,128]{2,1,0:T(8,128)(2,1)} %bitcast.21), custom_call_target="tpu_custom_call" | custom-call | tf_op jit(solution)/shard_map/prepare/pallas_call | solution.py:535
  16.5 0.0 collective-permute-done.2.refs_3_
  16.5 0.0 collective-permute-done.1.refs_2_
  16.5 0.0 collective-permute-done.refs_1_
  16.5 0.8 %all-to-all-done.arrived = bf16[8,80,128]{2,1,0:T(8,128)(2,1)S(1)} async-done(((bf16[8,80,128]{2,1,0:T(8,128)(2,1)}), bf16[8,80,128]{2,1,0:T(8,128)(2,1)S(1)}, u32[]{:S(2)}, u32[]{:S(2)}) %all-to-all-start) | async-done | bytes 163872 | tf_op jit(solution)/shard_map/all_to_all | solution.py:530
  17.2 0.0 copy-done
  17.3 0.0 copy-done.1
  17.3 8.3 %score.1 = (f32[8,16,128]{2,1,0:T(8,128)S(1)}, f32[4,72,128]{2,1,0:T(8,128)S(1)}, s32[1,280]{1,0:T(1,128)S(1)}, s32[1,1]{1,0:T(1,128)}, bf16[256,192,128]{2,1,0:T(8,128)(2,1)}) custom-call(bf16[8,80,128]{2,1,0:T(8,128)(2,1)S(1)} %all-to-all-done.arrived, s32[1,64]{1,0:T(1,128)S(1)} %bitcast.18, f32[1,2]{1,0:T(1,128)S(1)} %bitcast.17, ...), custom_call_target="tpu_custom_call" | custom-call | tf_op jit(solution)/shard_map/score/pallas_call | solution.py:548
  25.6 13.0 %all_to_all.15.scores = f32[8,16,128]{2,1,0:T(8,128)S(1)} all-to-all(f32[8,16,128]{2,1,0:T(8,128)S(1)} %get-tuple-element.12), channel_id=1, replica_groups=mesh['grp'=8,'rep'=4] {'grp'}, dimensions={0} | all-to-all | bytes 131072 | tf_op jit(solution)/shard_map/all_to_all | solution.py:579
  38.5 8.5 %query_grad.1 = (bf16[8,64,128]{2,1,0:T(8,128)(2,1)}, f32[4,72,128]{2,1,0:T(8,128)S(1)}, f32[1,128]{1,0:T(1,128)S(1)}, f32[1,128]{1,0:T(1,128)S(1)}) custom-call(bf16[8,80,128]{2,1,0:T(8,128)(2,1)S(1)} %all-to-all-done.arrived, f32[8,16,128]{2,1,0:T(8,128)S(1)} %all_to_all.15.scores, f32[4,72,128]{2,1,0:T(8,128)S(1)} %get-tuple-element.13.summed, ...), custom_call_target="tpu_custom_call" | custom-call | tf_op jit(solution)/shard_map/query_grad/pallas_call | solution.py:582
  47.0 0.8 %collective-permute-start.5 = (f32[1,128]{1,0:T(1,128)S(1)}, f32[1,128]{1,0:T(1,128)S(1)}, u32[]{:S(2)}, u32[]{:S(2)}) collective-permute-start(f32[1,128]{1,0:T(1,128)S(1)} %get-tuple-element.17), channel_id=1, source_target_pairs={{0,3},{1,2},{2,1},{3,0},{4,7},{5,6},{6,5},{7,4},{8,11},{9,10},{10,... | collective-permute-start | bytes 1544 | tf_op jit(solution)/shard_map/ppermute | solution.py:490
  47.9 1.4 %collective-permute-start.4 = (f32[1,128]{1,0:T(1,128)S(1)}, f32[1,128]{1,0:T(1,128)S(1)}, u32[]{:S(2)}, u32[]{:S(2)}) collective-permute-start(f32[1,128]{1,0:T(1,128)S(1)} %get-tuple-element.17), channel_id=1, source_target_pairs={{0,2},{1,3},{2,0},{3,1},{4,6},{5,7},{6,4},{7,5},{8,10},{9,11},{10,... | collective-permute-start | bytes 1544 | tf_op jit(solution)/shard_map/ppermute | solution.py:490
  49.2 0.0 collective-permute-start.3
  49.3 4.4 %all-to-all-start.2 = ((bf16[8,64,128]{2,1,0:T(8,128)(2,1)}), bf16[8,64,128]{2,1,0:T(8,128)(2,1)S(1)}, u32[]{:S(2)}, u32[]{:S(2)}) async-start(bf16[8,64,128]{2,1,0:T(8,128)(2,1)} %get-tuple-element.19), calls=%async_computation.2 | async-start | bytes 262144 | tf_op jit(solution)/shard_map/all_to_all | solution.py:602
  53.6 6.6 %passage_grad.1 = bf16[180,64,128]{2,1,0:T(8,128)(2,1)} custom-call(bf16[8,80,128]{2,1,0:T(8,128)(2,1)S(1)} %all-to-all-done.arrived, f32[4,72,128]{2,1,0:T(8,128)S(1)} %get-tuple-element.20.multiplier, s32[1,280]{1,0:T(1,128)S(1)} %get-tuple-element.14.block_code, s32[1,1]{1,0:T(1,128)} %get-tuple-element.15.block_count, ...), custom_call_target="tpu_custom_call" | custom-call | flops 1610612736 | bytes 12582912 | tf_op jit(solution)/shard_map/passage_grad/pallas_call | solution.py:604
  60.2 0.0 collective-permute-done.5
  60.2 0.0 collective-permute-done.4
  60.3 0.0 collective-permute-done.3
  60.4 0.9 %all-to-all-done.2 = bf16[8,64,128]{2,1,0:T(8,128)(2,1)S(1)} async-done(((bf16[8,64,128]{2,1,0:T(8,128)(2,1)}), bf16[8,64,128]{2,1,0:T(8,128)(2,1)S(1)}, u32[]{:S(2)}, u32[]{:S(2)}) %all-to-all-start.2) | async-done | bytes 131104 | tf_op jit(solution)/shard_map/all_to_all | solution.py:602
  61.2 0.6 %convert_reduce_fusion = f32[64,128]{1,0:T(8,128)} fusion(bf16[8,64,128]{2,1,0:T(8,128)(2,1)S(1)} %all-to-all-done.2), kind=kLoop, calls=%fused_computation | loop fusion | flops 122880 | bytes 163840 | tf_op jit(solution)/shard_map/reduce_sum | solution.py:628
  (1 shorter events, 0.0 us)
Async XLA Ops:
  2.2 15.0 %copy-start = (f32[2,1]{0,1:T(1,128)S(1)}, f32[2,1]{0,1:T(1,128)}, u32[]{:S(2)}) copy-start(f32[2,1]{0,1:T(1,128)} %param.13) | copy-start | bytes 28
  2.2 15.0 %copy-start.1 = (s32[64,1]{0,1:T(1,128)S(1)}, s32[64,1]{0,1:T(1,128)}, u32[]{:S(2)}) copy-start(s32[64,1]{0,1:T(1,128)} %param.9) | copy-start | bytes 772
  2.2 15.0 %all-to-all-start = ((bf16[8,80,128]{2,1,0:T(8,128)(2,1)}), bf16[8,80,128]{2,1,0:T(8,128)(2,1)S(1)}, u32[]{:S(2)}, u32[]{:S(2)}) async-start(bf16[8,80,128]{2,1,0:T(8,128)(2,1)} %pack.1), calls=%async_computation | async-start | bytes 327680 | tf_op jit(solution)/shard_map/all_to_all | solution.py:530
  9.7 6.8 %collective-permute-start.2 = (f32[1,2]{1,0:T(1,128)}, f32[1,2]{1,0:T(1,128)S(1)}, u32[]{:S(2)}, u32[]{:S(2)}) collective-permute-start(f32[1,2]{1,0:T(1,128)} %bitcast.14), channel_id=1, source_target_pairs={{0,3},{1,2},{2,1},{3,0},{4,7},{5,6},{6,5},{7,4},{8,11},{9,10},{10,... | collective-permute-start | bytes 32 | tf_op jit(solution)/shard_map/ppermute | solution.py:490
  10.3 6.2 %collective-permute-start.1 = (f32[1,2]{1,0:T(1,128)}, f32[1,2]{1,0:T(1,128)S(1)}, u32[]{:S(2)}, u32[]{:S(2)}) collective-permute-start(f32[1,2]{1,0:T(1,128)} %bitcast.15), channel_id=1, source_target_pairs={{0,2},{1,3},{2,0},{3,1},{4,6},{5,7},{6,4},{7,5},{8,10},{9,11},{10,... | collective-permute-start | bytes 32 | tf_op jit(solution)/shard_map/ppermute | solution.py:490
  11.3 5.2 %collective-permute-start = (f32[1,2]{1,0:T(1,128)}, f32[1,2]{1,0:T(1,128)S(1)}, u32[]{:S(2)}, u32[]{:S(2)}) collective-permute-start(f32[1,2]{1,0:T(1,128)} %bitcast.16), channel_id=1, source_target_pairs={{0,1},{1,0},{2,3},{3,2},{4,5},{5,4},{6,7},{7,6},{8,9},{9,8},{10,11... | collective-permute-start | bytes 32 | tf_op jit(solution)/shard_map/ppermute | solution.py:490
  47.0 13.2 %collective-permute-start.5 = (f32[1,128]{1,0:T(1,128)S(1)}, f32[1,128]{1,0:T(1,128)S(1)}, u32[]{:S(2)}, u32[]{:S(2)}) collective-permute-start(f32[1,128]{1,0:T(1,128)S(1)} %get-tuple-element.17), channel_id=1, source_target_pairs={{0,3},{1,2},{2,1},{3,0},{4,7},{5,6},{6,5},{7,4},{8,11},{9,10},{10,... | collective-permute-start | bytes 1544 | tf_op jit(solution)/shard_map/ppermute | solution.py:490
  47.9 12.4 %collective-permute-start.4 = (f32[1,128]{1,0:T(1,128)S(1)}, f32[1,128]{1,0:T(1,128)S(1)}, u32[]{:S(2)}, u32[]{:S(2)}) collective-permute-start(f32[1,128]{1,0:T(1,128)S(1)} %get-tuple-element.17), channel_id=1, source_target_pairs={{0,2},{1,3},{2,0},{3,1},{4,6},{5,7},{6,4},{7,5},{8,10},{9,11},{10,... | collective-permute-start | bytes 1544 | tf_op jit(solution)/shard_map/ppermute | solution.py:490
  49.2 11.0 %collective-permute-start.3 = (f32[1,128]{1,0:T(1,128)S(1)}, f32[1,128]{1,0:T(1,128)S(1)}, u32[]{:S(2)}, u32[]{:S(2)}) collective-permute-start(f32[1,128]{1,0:T(1,128)S(1)} %get-tuple-element.17), channel_id=1, source_target_pairs={{0,1},{1,0},{2,3},{3,2},{4,5},{5,4},{6,7},{7,6},{8,9},{9,8},{10,11... | collective-permute-start | bytes 1544 | tf_op jit(solution)/shard_map/ppermute | solution.py:490
  49.3 12.0 %all-to-all-start.2 = ((bf16[8,64,128]{2,1,0:T(8,128)(2,1)}), bf16[8,64,128]{2,1,0:T(8,128)(2,1)S(1)}, u32[]{:S(2)}, u32[]{:S(2)}) async-start(bf16[8,64,128]{2,1,0:T(8,128)(2,1)} %get-tuple-element.19), calls=%async_computation.2 | async-start | bytes 262144 | tf_op jit(solution)/shard_map/all_to_all | solution.py:602

commit v2 on v1

--- a/solution.py
+++ b/solution.py
@@ -15,6 +15,7 @@
 KINDS = 8
 UNROLL = 8
 SPREAD = 4
+SUMS = 4
 STORE = 5
 PIECES = 4
 HIGHEST = lax.Precision.HIGHEST
@@ -74,13 +75,17 @@
     return jnp.where(owner == me.astype(jnp.float32), local, -1.0).astype(jnp.int32)
 
 
-def prepare_kernel(stored, rows_out, gathered):
+def prepare_kernel(stored, rows_out, turned_out, gathered):
     token_len, chunk, feature = stored.shape
     padded = rows_out.shape[1]
     pitch = gathered.shape[0] // chunk
-    for p in range(chunk):
-        at = p * pitch + token_len
-        gathered[at : (p + 1) * pitch, :] = jnp.zeros((pitch - token_len, feature), jnp.float32)
+
+    def clear(p, carry):
+        at = pl.ds(p * pitch + token_len, padded - token_len)
+        gathered[at, :] = jnp.zeros((padded - token_len, feature), jnp.float32)
+        return carry
+
+    lax.fori_loop(0, chunk, clear, 0)
 
     def spread(j, carry):
         for u in range(SPREAD):
@@ -92,8 +97,17 @@
     for j in range(token_len - token_len % SPREAD, token_len):
         gathered[pl.ds(j, chunk, stride=pitch), :] = stored[j].astype(jnp.float32)
 
-    for p in range(chunk):
-        rows_out[p] = gathered[p * pitch : p * pitch + padded, :].astype(jnp.bfloat16)
+    ahead = math.gcd(chunk, 8)
+
+    def collect(step, carry):
+        for inner in range(ahead):
+            p = step * ahead + inner
+            block = gathered[pl.ds(p * pitch, padded), :].astype(jnp.bfloat16)
+            rows_out[p] = block
+            turned_out[p, :, 0:padded] = block.T
+        return carry
+
+    lax.fori_loop(0, chunk // ahead, collect, 0)
 
 
 def list_blocks(flags_scalar, block_code, block_count, passage_count, tiles):
@@ -135,14 +149,14 @@
 ):
     tokens, query_local, candidates, per_tile, replicas = dims
     weights, refs = refs[:replicas], refs[replicas:]
-    passages_hbm, scores_out, summed, block_code, block_count, powers_hbm, *scratch = refs
+    passages, scores_out, summed, block_code, block_count, powers_hbm, *scratch = refs
     score_body(
         (tokens, query_local, candidates, per_tile),
         lax.axis_index(axis),
         arrived,
         lengths,
         pair_sums([one[...] for one in weights]),
-        passages_hbm,
+        passages,
         scores_out,
         summed,
         block_code,
@@ -158,14 +172,13 @@
     arrived,
     lengths,
     weights,
-    passages_hbm,
+    passages,
     scores_out,
     summed,
     block_code,
     block_count,
     powers_hbm,
     highest,
-    passages,
     turned,
     flags,
     flags_scalar,
@@ -176,7 +189,6 @@
     odd_top,
     powers,
     flags_done,
-    rows_done,
     powers_done,
 ):
     tokens, query_local, candidates, per_tile = dims
@@ -184,8 +196,6 @@
     passage_count, padded, _ = passages.shape
     tiles, _, lanes = highest.shape
     groups_per_tile = per_tile // query_local
-    fetch_rows = pltpu.make_async_copy(passages_hbm, passages, rows_done)
-    fetch_rows.start()
 
     column = iota(flags.shape, 1)
     passage_index = iota((passage_count, candidates), 0)
@@ -214,7 +224,6 @@
     penalty[...] = jnp.where(iota(penalty.shape, 0) < padded, 0.0, MASKED)
     to_scalar.wait()
     steps = list_blocks(flags_scalar, block_code, block_count, passage_count, tiles)
-    fetch_rows.wait()
 
     factor = LOG2E / TEMPER
 
@@ -292,32 +301,29 @@
     arrived,
     scores,
     summed,
+    turned,
     block_code,
     block_count,
-    passages_hbm,
     powers_hbm,
     grads_out,
     multiplier,
     numerator_out,
     weight_sum_out,
-    passages,
     powers,
-    sums,
-    rows_done,
+    factors,
     powers_done,
+    *sums,
 ):
     tokens, query_local, candidates, per_tile, query_total = dims
     groups = arrived.shape[0]
     tiles, slots, lanes = summed.shape
-    passage_count, _, _ = passages.shape
+    passage_count = turned.shape[0]
+    padded = powers.shape[1]
     groups_per_tile = per_tile // query_local
     queries_all = tiles * per_tile
     query_len = lanes // per_tile
     me = lax.axis_index(axis)
     steps = block_count[0, 0]
-
-    fetch_rows = pltpu.make_async_copy(passages_hbm, passages, rows_done)
-    fetch_rows.start()
 
     def chunk_copy(s):
         at = pl.ds(s * 2 * UNROLL, 2 * UNROLL)
@@ -370,11 +376,12 @@
             picked = jnp.where(passage_index == mine, grad[at : at + 1], 0.0)
             total = jnp.sum(picked, axis=1, keepdims=True)
             spread_out = jnp.where(lane_query == inner, total, spread_out)
-        multiplier[tile, 0:passage_count, :] = spread_out / summed[tile, 0:passage_count, :]
-        multiplier[tile, passage_count:, :] = jnp.zeros((slots - passage_count, lanes), jnp.float32)
-
-    sums[...] = jnp.zeros_like(sums)
-    fetch_rows.wait()
+        factors[tile, 0:passage_count, :] = spread_out / summed[tile, 0:passage_count, :]
+        factors[tile, passage_count:, :] = jnp.zeros((slots - passage_count, lanes), jnp.float32)
+    multiplier[...] = factors[...]
+
+    for one in sums:
+        one[...] = jnp.zeros_like(one)
 
     def step(s, carry):
         chunk_copy(s).wait()
@@ -382,16 +389,16 @@
             b = s * 2 * UNROLL + u
             slot, tile = decode(block_code, b, tiles)
             p = jnp.minimum(slot, passage_count - 1)
-            part = powers[b].astype(jnp.float32) * multiplier[tile, pl.ds(slot, 1), :]
+            part = powers[b].astype(jnp.float32) * factors[tile, pl.ds(slot, 1), :]
             part = part.astype(jnp.bfloat16)
-            sums[tile] += lax.dot_general(
-                passages[p], part, (((0,), (0,)), ((), ())), preferred_element_type=jnp.float32
+            sums[u % len(sums)][tile] += jnp.dot(
+                turned[p, :, 0:padded], part, preferred_element_type=jnp.float32
             )
         return carry
 
     lax.fori_loop(0, steps, step, 0)
     for tile in range(tiles):
-        back = sums[tile].T.astype(jnp.bfloat16)
+        back = pair_sums([one[tile] for one in sums]).T.astype(jnp.bfloat16)
         for inner in range(groups_per_tile):
             g = tile * groups_per_tile + inner
             grads_out[g] = back[inner * tokens : (inner + 1) * tokens]
@@ -516,7 +523,7 @@
     score_rows = round_up(groups * query_local, 8)
     shape = jax.ShapeDtypeStruct
     alone = pltpu.CompilerParams(vmem_limit_bytes=62 * 2**20)
-    params = pltpu.CompilerParams(vmem_limit_bytes=52 * 2**20)
+    params = pltpu.CompilerParams(vmem_limit_bytes=48 * 2**20)
 
     share = pl.pallas_call(
         functools.partial(pack_kernel, passage_local),
@@ -531,14 +538,15 @@
 
     replica_weights = from_replicas(weights.T, replicas)
 
-    chunk = math.gcd(passage_local, 16)
-    rows = pl.pallas_call(
+    rows, turned = pl.pallas_call(
         prepare_kernel,
-        grid=(passage_local // chunk,),
-        out_shape=shape((passage_local, padded, feature), jnp.bfloat16),
-        in_specs=[pl.BlockSpec((token_len, chunk, feature), lambda i: (0, i, 0))],
-        out_specs=pl.BlockSpec((chunk, padded, feature), lambda i: (i, 0, 0)),
-        scratch_shapes=[VMEM((chunk * pitch, feature), jnp.float32)],
+        out_shape=(
+            shape((passage_local, padded, feature), jnp.bfloat16),
+            shape((passage_local, feature, round_up(padded, 128)), jnp.bfloat16),
+        ),
+        in_specs=vmem(1),
+        out_specs=tuple(vmem(2)),
+        scratch_shapes=[VMEM((passage_local * pitch, feature), jnp.float32)],
         name="prepare",
         compiler_params=params,
     )(passages[:, 0].transpose(1, 0, 2))
@@ -554,11 +562,10 @@
                 shape((1, 1), jnp.int32),
                 shape((chunks * 2 * UNROLL, padded, lanes), jnp.bfloat16),
             ),
-            in_specs=vmem(1) + smem(1) + vmem(replicas) + hbm(1),
+            in_specs=vmem(1) + smem(1) + vmem(replicas + 1),
             out_specs=tuple(vmem(2) + smem(2) + hbm(1)),
             scratch_shapes=[
                 VMEM((tiles, slots, lanes), jnp.float32),
-                VMEM((passage_local, padded, feature), jnp.bfloat16),
                 VMEM((tiles, feature, lanes), jnp.bfloat16),
                 VMEM((passage_local, 128), jnp.int32),
                 SMEM((passage_local, 128), jnp.int32),
@@ -569,7 +576,6 @@
                 VMEM((UNROLL, lanes), jnp.float32),
                 VMEM((chunks * 2 * UNROLL, padded, lanes), jnp.bfloat16),
                 pltpu.SemaphoreType.DMA,
-                pltpu.SemaphoreType.DMA,
                 pltpu.SemaphoreType.DMA((chunks,)),
             ],
             name="score",
@@ -587,18 +593,17 @@
             shape((1, 128), jnp.float32),
             shape((1, 128), jnp.float32),
         ),
-        in_specs=vmem(3) + smem(2) + hbm(2),
+        in_specs=vmem(4) + smem(2) + hbm(1),
         out_specs=tuple(vmem(4)),
         scratch_shapes=[
-            VMEM(rows.shape, jnp.bfloat16),
             VMEM(powers.shape, jnp.bfloat16),
-            VMEM((tiles, feature, lanes), jnp.float32),
-            pltpu.SemaphoreType.DMA,
+            VMEM((tiles, slots, lanes), jnp.float32),
             pltpu.SemaphoreType.DMA((chunks,)),
-        ],
+        ]
+        + [VMEM((tiles, feature, lanes), jnp.float32)] * SUMS,
         name="query_grad",
         compiler_params=params,
-    )(arrived, all_scores, summed, block_code, block_count, rows, powers)
+    )(arrived, all_scores, summed, turned, block_code, block_count, powers)
     returned = lax.all_to_all(grads, "grp", split_axis=0, concat_axis=0, tiled=True)
 
     passage_grad = pl.pallas_call(

time: 63.5 us -> 63.3 us (level)
  local copies, waits for them, and re-layouts: 0.01 us -> 4.03 us
  Pallas kernels: 30 us -> 26.6 us
  starting transfers between devices: 15.9 us -> 14.8 us
  blocking collectives: 13 us -> 13.7 us
    unnamed x4 -> x8, local copies, waits for them, and re-layouts: 0.01 us -> 4.03 us
    pallas_call x1, Pallas kernels: 8.5 us -> 5.91 us  [on_device(): pl.pallas_call(functools.partial(query_kernel, dims + (query_total,), 'gr...]
    all_to_all x1, starting transfers between devices: 4.36 us -> 3.37 us  [on_device(): lax.all_to_all(grads, 'grp', split_axis=0, concat_axis=0, tiled=True)]
    all_to_all x1, waiting for transfers between devices: 0.75 us -> 0.01 us  [on_device(): lax.all_to_all(share, 'grp', split_axis=0, concat_axis=0, tiled=True)]
    all_to_all x1, blocking collectives: 13 us -> 13.7 us  [on_device(): lax.all_to_all(scores, 'grp', split_axis=0, concat_axis=0, tiled=True)]
  transfers between devices with their start and end apart: 8 -> 8, of which waited for: 2 -> 1; matrix products, arithmetic and copies ran while one was open for 0% -> 0% of each run, Pallas kernels for 18% -> 18%
where the time goes in v2:
time: 63.3 us; the launch traced here: 62.8 us
  Pallas kernels  26.6 us (42%)
  starting transfers between devices  14.8 us (23%)
  blocking collectives  13.7 us (22%)
  local copies, waits for them, and re-layouts  4.03 us (6%)
  between operations  1.96 us (3%)
  waiting for transfers between devices  1.11 us (2%)
  other arithmetic  0.64 us (1%)
    all_to_all x1, blocking collectives, on_device(): lax.all_to_all(scores, 'grp', split_axis=0, concat_axis=0, tiled=True)  13.7 us
    pallas_call x1, Pallas kernels, on_device(): pl.pallas_call(functools.partial(score_kernel, dims + (replicas,), 'grp')...  8.02 us
    all_to_all x1, starting transfers between devices, on_device(): lax.all_to_all(share, 'grp', split_axis=0, concat_axis=0, tiled=True)  7.31 us
    pallas_call x1, Pallas kernels, on_device(): pl.pallas_call(functools.partial(passage_kernel, (tokens, per_tile // que...  6.61 us
    pallas_call x1, Pallas kernels, on_device(): pl.pallas_call(functools.partial(query_kernel, dims + (query_total,), 'gr...  5.91 us
    pallas_call x1, Pallas kernels, on_device(): pl.pallas_call(prepare_kernel, out_shape=(shape((passage_local, padded, f...  4.41 us
    ppermute x6, starting transfers between devices, from_replicas(): return [values] + [lax.ppermute(values, 'rep', ring) for ring in rings]  4.09 us
    unnamed x8, local copies, waits for them, and re-layouts  4.03 us
  transfers between devices with their start and end apart: 8, of which 1 were waited for; matrix products, arithmetic and copies ran while one was open for 0% of the time, Pallas kernels for 18%

profile of v2, /device:TPU:0, one launch (start us, length us, event | category | flops | bytes accessed | tf_op | source)
XLA Modules:
  0.0 62.8 jit_solution(7993461068663028516)
XLA Ops:
  0.6 0.0 copy-start.2
  0.6 0.0 copy-start.3
  0.7 1.6 %pack.1 = bf16[8,80,128]{2,1,0:T(8,128)(2,1)} custom-call(bf16[64,128]{1,0:T(8,128)(2,1)} %bitcast.23, s32[2,1,64]{2,1,0:T(1,128)} %cand_ids.1, s32[1,512]{1,0:T(1,128)} %owner_map.1, f32[2,1,64]{2,1,0:T(1,128)} %teacher.1, f32[1,2]{1,0:T(1,128)} %bitcast.14), custom_call_target="tpu_custom_call" | custom-call | tf_op jit(solution)/shard_map/pack/pallas_call | solution.py:528
  2.3 7.3 %all-to-all-start = ((bf16[8,80,128]{2,1,0:T(8,128)(2,1)}), bf16[8,80,128]{2,1,0:T(8,128)(2,1)S(1)}, u32[]{:S(2)}, u32[]{:S(2)}) async-start(bf16[8,80,128]{2,1,0:T(8,128)(2,1)} %pack.1), calls=%async_computation | async-start | bytes 327680 | tf_op jit(solution)/shard_map/all_to_all | solution.py:537
  9.6 0.7 %collective-permute-start.2 = (f32[1,2]{1,0:T(1,128)}, f32[1,2]{1,0:T(1,128)S(1)}, u32[]{:S(2)}, u32[]{:S(2)}) collective-permute-start(f32[1,2]{1,0:T(1,128)} %bitcast.15), channel_id=1, source_target_pairs={{0,3},{1,2},{2,1},{3,0},{4,7},{5,6},{6,5},{7,4},{8,11},{9,10},{10,... | collective-permute-start | bytes 32 | tf_op jit(solution)/shard_map/ppermute | solution.py:497
  10.2 0.9 %collective-permute-start.1 = (f32[1,2]{1,0:T(1,128)}, f32[1,2]{1,0:T(1,128)S(1)}, u32[]{:S(2)}, u32[]{:S(2)}) collective-permute-start(f32[1,2]{1,0:T(1,128)} %bitcast.16), channel_id=1, source_target_pairs={{0,2},{1,3},{2,0},{3,1},{4,6},{5,7},{6,4},{7,5},{8,10},{9,11},{10,... | collective-permute-start | bytes 32 | tf_op jit(solution)/shard_map/ppermute | solution.py:497
  11.2 0.3 collective-permute-start
  11.4 0.0 copy-start.1
  11.4 1.8 %copy-done.1 = bf16[64,1,180,128]{3,0,2,1:T(8,128)(2,1)S(1)} copy-done((bf16[64,1,180,128]{3,0,2,1:T(8,128)(2,1)S(1)}, bf16[64,1,180,128]{3,0,2,1:T(8,128)(2,1)}, u32[]{:S(2)}) %copy-start.1) | copy-done | bytes 2949144
  13.3 4.4 %prepare.1 = (bf16[64,192,128]{2,1,0:T(8,128)(2,1)S(1)}, bf16[64,128,256]{2,1,0:T(8,128)(2,1)}) custom-call(bf16[180,64,128]{2,1,0:T(8,128)(2,1)S(1)} %bitcast.13), custom_call_target="tpu_custom_call" | custom-call | tf_op jit(solution)/shard_map/prepare/pallas_call | solution.py:541
  17.7 0.0 collective-permute-done.2.refs_3_
  17.7 0.0 collective-permute-done.1.refs_2_
  17.7 0.0 collective-permute-done.refs_1_
  17.7 0.0 all-to-all-done.arrived
  17.7 0.0 copy-done.2
  17.7 0.0 copy-done.3
  17.7 8.0 %score.1 = (f32[8,16,128]{2,1,0:T(8,128)S(1)}, f32[4,72,128]{2,1,0:T(8,128)S(1)}, s32[1,280]{1,0:T(1,128)S(1)}, s32[1,1]{1,0:T(1,128)}, bf16[256,192,128]{2,1,0:T(8,128)(2,1)}) custom-call(bf16[8,80,128]{2,1,0:T(8,128)(2,1)S(1)} %all-to-all-done.arrived, s32[1,64]{1,0:T(1,128)S(1)} %bitcast.19, f32[1,2]{1,0:T(1,128)S(1)} %bitcast.18, ...), custom_call_target="tpu_custom_call" | custom-call | tf_op jit(solution)/shard_map/score/pallas_call | solution.py:556
  25.8 13.7 %all_to_all.15.scores = f32[8,16,128]{2,1,0:T(8,128)S(1)} all-to-all(f32[8,16,128]{2,1,0:T(8,128)S(1)} %get-tuple-element.15), channel_id=1, replica_groups=mesh['grp'=8,'rep'=4] {'grp'}, dimensions={0} | all-to-all | bytes 131072 | tf_op jit(solution)/shard_map/all_to_all | solution.py:585
  39.5 0.0 copy-start
  39.5 2.2 %copy-done = bf16[64,128,256]{2,1,0:T(8,128)(2,1)S(1)} copy-done((bf16[64,128,256]{2,1,0:T(8,128)(2,1)S(1)}, bf16[64,128,256]{2,1,0:T(8,128)(2,1)}, u32[]{:S(2)}) %copy-start) | copy-done | bytes 4194328
  41.7 5.9 %query_grad.1 = (bf16[8,64,128]{2,1,0:T(8,128)(2,1)}, f32[4,72,128]{2,1,0:T(8,128)S(1)}, f32[1,128]{1,0:T(1,128)S(1)}, f32[1,128]{1,0:T(1,128)S(1)}) custom-call(bf16[8,80,128]{2,1,0:T(8,128)(2,1)S(1)} %all-to-all-done.arrived, f32[8,16,128]{2,1,0:T(8,128)S(1)} %all_to_all.15.scores, f32[4,72,128]{2,1,0:T(8,128)S(1)} %get-tuple-element.16.summed, ...), custom_call_target="tpu_custom_call" | custom-call | tf_op jit(solution)/shard_map/query_grad/pallas_call | solution.py:588
  47.6 0.5 collective-permute-start.5
  48.1 1.7 %collective-permute-start.4 = (f32[1,128]{1,0:T(1,128)S(1)}, f32[1,128]{1,0:T(1,128)S(1)}, u32[]{:S(2)}, u32[]{:S(2)}) collective-permute-start(f32[1,128]{1,0:T(1,128)S(1)} %get-tuple-element.21), channel_id=1, source_target_pairs={{0,2},{1,3},{2,0},{3,1},{4,6},{5,7},{6,4},{7,5},{8,10},{9,11},{10,... | collective-permute-start | bytes 1544 | tf_op jit(solution)/shard_map/ppermute | solution.py:497
  49.8 0.0 collective-permute-start.3
  49.8 3.4 %all-to-all-start.2 = ((bf16[8,64,128]{2,1,0:T(8,128)(2,1)}), bf16[8,64,128]{2,1,0:T(8,128)(2,1)S(1)}, u32[]{:S(2)}, u32[]{:S(2)}) async-start(bf16[8,64,128]{2,1,0:T(8,128)(2,1)} %get-tuple-element.23), calls=%async_computation.2 | async-start | bytes 262144 | tf_op jit(solution)/shard_map/all_to_all | solution.py:607
  53.2 6.6 %passage_grad.1 = bf16[180,64,128]{2,1,0:T(8,128)(2,1)} custom-call(bf16[8,80,128]{2,1,0:T(8,128)(2,1)S(1)} %all-to-all-done.arrived, f32[4,72,128]{2,1,0:T(8,128)S(1)} %get-tuple-element.24.multiplier, s32[1,280]{1,0:T(1,128)S(1)} %get-tuple-element.18.block_code, s32[1,1]{1,0:T(1,128)} %get-tuple-element.19.block_count, ...), custom_call_target="tpu_custom_call" | custom-call | flops 1610612736 | bytes 12582912 | tf_op jit(solution)/shard_map/passage_grad/pallas_call | solution.py:609
  59.8 0.0 collective-permute-done.5
  59.8 0.0 collective-permute-done.4
  59.8 0.0 collective-permute-done.3
  59.9 1.1 %all-to-all-done.2 = bf16[8,64,128]{2,1,0:T(8,128)(2,1)S(1)} async-done(((bf16[8,64,128]{2,1,0:T(8,128)(2,1)}), bf16[8,64,128]{2,1,0:T(8,128)(2,1)S(1)}, u32[]{:S(2)}, u32[]{:S(2)}) %all-to-all-start.2) | async-done | bytes 131104 | tf_op jit(solution)/shard_map/all_to_all | solution.py:607
  61.0 0.6 %convert_reduce_fusion = f32[64,128]{1,0:T(8,128)} fusion(bf16[8,64,128]{2,1,0:T(8,128)(2,1)S(1)} %all-to-all-done.2), kind=kLoop, calls=%fused_computation | loop fusion | flops 122880 | bytes 163840 | tf_op jit(solution)/shard_map/reduce_sum | solution.py:633
  (1 shorter events, 0.0 us)
Async XLA Ops:
  0.6 17.1 %copy-start.2 = (f32[2,1]{0,1:T(1,128)S(1)}, f32[2,1]{0,1:T(1,128)}, u32[]{:S(2)}) copy-start(f32[2,1]{0,1:T(1,128)} %param.13) | copy-start | bytes 28
  0.6 17.1 %copy-start.3 = (s32[64,1]{0,1:T(1,128)S(1)}, s32[64,1]{0,1:T(1,128)}, u32[]{:S(2)}) copy-start(s32[64,1]{0,1:T(1,128)} %param.9) | copy-start | bytes 772
  2.3 15.4 %all-to-all-start = ((bf16[8,80,128]{2,1,0:T(8,128)(2,1)}), bf16[8,80,128]{2,1,0:T(8,128)(2,1)S(1)}, u32[]{:S(2)}, u32[]{:S(2)}) async-start(bf16[8,80,128]{2,1,0:T(8,128)(2,1)} %pack.1), calls=%async_computation | async-start | bytes 327680 | tf_op jit(solution)/shard_map/all_to_all | solution.py:537
  9.6 8.1 %collective-permute-start.2 = (f32[1,2]{1,0:T(1,128)}, f32[1,2]{1,0:T(1,128)S(1)}, u32[]{:S(2)}, u32[]{:S(2)}) collective-permute-start(f32[1,2]{1,0:T(1,128)} %bitcast.15), channel_id=1, source_target_pairs={{0,3},{1,2},{2,1},{3,0},{4,7},{5,6},{6,5},{7,4},{8,11},{9,10},{10,... | collective-permute-start | bytes 32 | tf_op jit(solution)/shard_map/ppermute | solution.py:497
  10.2 7.5 %collective-permute-start.1 = (f32[1,2]{1,0:T(1,128)}, f32[1,2]{1,0:T(1,128)S(1)}, u32[]{:S(2)}, u32[]{:S(2)}) collective-permute-start(f32[1,2]{1,0:T(1,128)} %bitcast.16), channel_id=1, source_target_pairs={{0,2},{1,3},{2,0},{3,1},{4,6},{5,7},{6,4},{7,5},{8,10},{9,11},{10,... | collective-permute-start | bytes 32 | tf_op jit(solution)/shard_map/ppermute | solution.py:497
  11.2 6.5 %collective-permute-start = (f32[1,2]{1,0:T(1,128)}, f32[1,2]{1,0:T(1,128)S(1)}, u32[]{:S(2)}, u32[]{:S(2)}) collective-permute-start(f32[1,2]{1,0:T(1,128)} %bitcast.17), channel_id=1, source_target_pairs={{0,1},{1,0},{2,3},{3,2},{4,5},{5,4},{6,7},{7,6},{8,9},{9,8},{10,11... | collective-permute-start | bytes 32 | tf_op jit(solution)/shard_map/ppermute | solution.py:497
  11.4 1.8 %copy-start.1 = (bf16[64,1,180,128]{3,0,2,1:T(8,128)(2,1)S(1)}, bf16[64,1,180,128]{3,0,2,1:T(8,128)(2,1)}, u32[]{:S(2)}) copy-start(bf16[64,1,180,128]{3,0,2,1:T(8,128)(2,1)} %param.8) | copy-start | bytes 8847364
  39.5 2.2 %copy-start = (bf16[64,128,256]{2,1,0:T(8,128)(2,1)S(1)}, bf16[64,128,256]{2,1,0:T(8,128)(2,1)}, u32[]{:S(2)}) copy-start(bf16[64,128,256]{2,1,0:T(8,128)(2,1)} %get-tuple-element.17.turned) | copy-start | bytes 12582916
  47.6 12.2 %collective-permute-start.5 = (f32[1,128]{1,0:T(1,128)S(1)}, f32[1,128]{1,0:T(1,128)S(1)}, u32[]{:S(2)}, u32[]{:S(2)}) collective-permute-start(f32[1,128]{1,0:T(1,128)S(1)} %get-tuple-element.21), channel_id=1, source_target_pairs={{0,3},{1,2},{2,1},{3,0},{4,7},{5,6},{6,5},{7,4},{8,11},{9,10},{10,... | collective-permute-start | bytes 1544 | tf_op jit(solution)/shard_map/ppermute | solution.py:497
  48.1 11.7 %collective-permute-start.4 = (f32[1,128]{1,0:T(1,128)S(1)}, f32[1,128]{1,0:T(1,128)S(1)}, u32[]{:S(2)}, u32[]{:S(2)}) collective-permute-start(f32[1,128]{1,0:T(1,128)S(1)} %get-tuple-element.21), channel_id=1, source_target_pairs={{0,2},{1,3},{2,0},{3,1},{4,6},{5,7},{6,4},{7,5},{8,10},{9,11},{10,... | collective-permute-start | bytes 1544 | tf_op jit(solution)/shard_map/ppermute | solution.py:497
  49.8 10.1 %collective-permute-start.3 = (f32[1,128]{1,0:T(1,128)S(1)}, f32[1,128]{1,0:T(1,128)S(1)}, u32[]{:S(2)}, u32[]{:S(2)}) collective-permute-start(f32[1,128]{1,0:T(1,128)S(1)} %get-tuple-element.21), channel_id=1, source_target_pairs={{0,1},{1,0},{2,3},{3,2},{4,5},{5,4},{6,7},{7,6},{8,9},{9,8},{10,11... | collective-permute-start | bytes 1544 | tf_op jit(solution)/shard_map/ppermute | solution.py:497
  49.8 11.2 %all-to-all-start.2 = ((bf16[8,64,128]{2,1,0:T(8,128)(2,1)}), bf16[8,64,128]{2,1,0:T(8,128)(2,1)S(1)}, u32[]{:S(2)}, u32[]{:S(2)}) async-start(bf16[8,64,128]{2,1,0:T(8,128)(2,1)} %get-tuple-element.23), calls=%async_computation.2 | async-start | bytes 262144 | tf_op jit(solution)/shard_map/all_to_all | solution.py:607
